TPU v7x, 8 devices: a whole 2x2x1 slice. The times are simulated.
8 devices in a mesh: data: 1 (over z), fsdp: 2 (over y), ep: 4 (over x, core).
Axes of the slice: x: 2, y: 2, z: 1, core: 2. Of those that a mesh axis runs over, the one named last changes fastest.
Arguments:
- tokens: bfloat16 [64, 512, 768], P(('data', 'fsdp', 'ep'))
- w_qkv: bfloat16 [768, 3, 12, 64], P('fsdp')
- w_out: bfloat16 [12, 64, 768], P(None, None, 'fsdp')
- w_gate: bfloat16 [8, 768, 3072], P('ep', 'fsdp')
- w_up: bfloat16 [8, 768, 3072], P('ep', 'fsdp')
- w_down: bfloat16 [8, 3072, 768], P('ep', None, 'fsdp')
- expert_idx: int32 [64, 512, 1], P(('data', 'fsdp', 'ep'))
- expert_slot: int32 [64, 512, 1], P(('data', 'fsdp', 'ep'))
- gate_wts: bfloat16 [64, 512, 1], P(('data', 'fsdp', 'ep'))
- d_out: bfloat16 [64, 512, 768], P(('data', 'fsdp', 'ep'))
Outputs:
- output 1: bfloat16 [64, 512, 768], P(('data', 'fsdp', 'ep'))
- output 2: bfloat16 [64, 512, 768], P(('data', 'fsdp', 'ep'))
- output 3: float32 [8, 768, 3072], P(('data', 'ep'), 'fsdp')
- output 4: float32 [8, 768, 3072], P(('data', 'ep'), 'fsdp')
- output 5: float32 [8, 3072, 768], P(('data', 'ep'), None, 'fsdp')
All inputs are finite; a program needn't handle non-finite values.
Results may differ from a plain program's by a relative error of at most 0.0149321.
Values are sent between devices in bfloat16 or wider.
A program may use at most 1 GiB of HBM per device.

v0:
```python
import functools

import jax
import jax.numpy as jnp
from jax import lax
from jax.experimental import pallas as pl
from jax.experimental.pallas import tpu as pltpu
from jax.sharding import PartitionSpec as P


F32 = jnp.float32
BF16 = jnp.bfloat16
TILE = 128
CHUNK_TILES = 5
CHUNK = TILE * CHUNK_TILES
PASS_TILES = 20
FF_STEP = 512
GROUP = ('fsdp', 'ep')
NN = (((1,), (0,)), ((), ()))
NT = (((1,), (1,)), ((), ()))
TN = (((0,), (0,)), ((), ()))


def mm(lhs, rhs, dims=NN):
    return lax.dot_general(lhs, rhs, dims, preferred_element_type=F32)


def params(limit_mib=60):
    return pltpu.CompilerParams(vmem_limit_bytes=limit_mib * 1024 * 1024)


ANY = pl.BlockSpec(memory_space=pl.ANY)
SMEM = pl.BlockSpec(memory_space=pltpu.SMEM)
VMEM = pl.BlockSpec(memory_space=pltpu.VMEM)


def route_kernel(n_exp, idx_ref, slot_ref, pos_ref, cnt_ref):
    idx, kept = idx_ref[...], slot_ref[...] >= 0
    rows, lanes = idx.shape
    upper = (lax.broadcasted_iota(jnp.int32, (lanes, lanes), 0) <= lax.broadcasted_iota(jnp.int32, (lanes, lanes), 1)).astype(F32).astype(BF16)
    lower = (lax.broadcasted_iota(jnp.int32, (rows, rows), 1) < lax.broadcasted_iota(jnp.int32, (rows, rows), 0)).astype(F32).astype(BF16)
    ones = jnp.ones((lanes, lanes), BF16)
    lane = lax.broadcasted_iota(jnp.int32, (1, lanes), 1)
    pos = jnp.full((rows, lanes), -1.0, F32)
    cnt = jnp.zeros((1, lanes), F32)
    off = jnp.zeros((1, 1), F32)
    for e in range(n_exp):
        mask = jnp.logical_and(idx == e, kept)
        wide = jnp.where(mask, 1.0, 0.0)
        mask_b = wide.astype(BF16)
        inside = mm(mask_b, upper)
        before = mm(lower, mm(mask_b, ones).astype(BF16))
        count = jnp.sum(jnp.sum(wide, axis=1, keepdims=True), axis=0, keepdims=True)
        pos = jnp.where(mask, off + before + inside - 1.0, pos)
        cnt = jnp.where(lane == e, count, cnt)
        off = off + jnp.floor((count + (TILE - 1.0)) * (1.0 / TILE)) * TILE
    pos_ref[...] = pos.astype(jnp.int32)
    cnt_ref[...] = cnt.astype(jnp.int32)


def route(idx, slot, n_exp):
    n = idx.size
    shape = (n // 128, 128)
    return pl.pallas_call(
        functools.partial(route_kernel, n_exp),
        out_shape=(jax.ShapeDtypeStruct(shape, jnp.int32), jax.ShapeDtypeStruct((1, 128), jnp.int32)),
        in_specs=[VMEM, VMEM],
        out_specs=(VMEM, VMEM),
        name='route',
    )(idx.reshape(shape), slot.reshape(shape))


PACK_STEP = 1024


def pack_kernel(weighted, c_ref, cnt_ref, pos_ref, gate_ref, x_ref, out_ref, acc_ref):
    k = pl.program_id(0)
    row = lax.broadcasted_iota(jnp.int32, (CHUNK, PACK_STEP), 0) + c_ref[0] * CHUNK
    hit = row == pos_ref[pl.ds(k, 1), :]
    value = gate_ref[pl.ds(k, 1), :] if weighted else 1.0
    part = mm(jnp.where(hit, value, 0.0).astype(BF16), x_ref[...])

    @pl.when(k == 0)
    def _():
        acc_ref[...] = part

    @pl.when(k > 0)
    def _():
        acc_ref[...] += part

    @pl.when(k == pl.num_programs(0) - 1)
    def _():
        out_ref[...] = acc_ref[...].astype(BF16)


def pack(chunk, counts, pos, gate, x, weighted):
    n, width = x.shape
    steps = n // PACK_STEP
    return pl.pallas_call(
        functools.partial(pack_kernel, weighted),
        grid=(steps,),
        out_shape=jax.ShapeDtypeStruct((CHUNK, width), BF16),
        in_specs=[SMEM, ANY, pl.BlockSpec((steps, PACK_STEP), lambda k: (0, 0)), pl.BlockSpec((steps, PACK_STEP), lambda k: (0, 0)), pl.BlockSpec((PACK_STEP, width), lambda k: (k, 0))],
        out_specs=pl.BlockSpec((CHUNK, width), lambda k: (0, 0)),
        scratch_shapes=[pltpu.VMEM((CHUNK, width), F32)],
        compiler_params=params(),
        cost_estimate=pl.CostEstimate(flops=2 * CHUNK * n * width, bytes_accessed=2 * n * width, transcendentals=0),
        name='pack',
    )(chunk.reshape(1), counts, pos.reshape(steps, PACK_STEP), gate, x)


UNPACK_STEP = 512


def unpack_kernel(weighted, n_ref, pos_ref, gate_ref, *refs):
    if weighted:
        h_ref, first_ref, more_ref, out_ref, buf, acc, sem = refs
    else:
        first_ref, more_ref, out_ref, buf, acc, sem = refs
    k = pl.program_id(0)
    pos = pos_ref[pl.ds(k, 1), :]
    row = lax.broadcasted_iota(jnp.int32, (CHUNK, UNPACK_STEP), 0)
    value = gate_ref[pl.ds(k, 1), :] if weighted else 1.0

    def gathered(base, rows):
        return mm(jnp.where(row + base == pos, value, 0.0).astype(BF16), rows, TN)

    acc[...] = gathered(0, first_ref[...])

    def more(c, carry):
        copy = pltpu.make_async_copy(more_ref.at[c - 1], buf, sem)
        copy.start()
        copy.wait()
        acc[...] += gathered(c * CHUNK, buf[...])
        return carry

    lax.fori_loop(1, n_ref[0], more, 0)
    total = acc[...]
    if weighted:
        total = h_ref[...].astype(F32) + total
    out_ref[...] = total.astype(BF16)


def unpack(n_chunks, pos, gate, h, first, more):
    weighted = h is not None
    n = pos.size
    width = first.shape[1]
    steps = n // UNPACK_STEP
    small = pl.BlockSpec((steps, UNPACK_STEP), lambda k: (0, 0))
    rows = pl.BlockSpec((UNPACK_STEP, width), lambda k: (k, 0))
    return pl.pallas_call(
        functools.partial(unpack_kernel, weighted),
        grid=(steps,),
        out_shape=jax.ShapeDtypeStruct((n, width), BF16),
        in_specs=[SMEM, small, small] + ([rows] if weighted else []) + [pl.BlockSpec((CHUNK, width), lambda k: (0, 0)), ANY],
        out_specs=rows,
        scratch_shapes=[pltpu.VMEM((CHUNK, width), BF16), pltpu.VMEM((UNPACK_STEP, width), F32), pltpu.SemaphoreType.DMA],
        compiler_params=params(),
        cost_estimate=pl.CostEstimate(flops=2 * CHUNK * n * width, bytes_accessed=4 * n * width, transcendentals=0),
        name='unpack',
    )(n_chunks.reshape(1), pos.reshape(steps, UNPACK_STEP), gate.reshape(steps, UNPACK_STEP), *([h] if weighted else []), first, more)


QUERY_BLOCK = 256


def load_attention_weights(w_hbm, wqkv, wo, sem):
    n_dev, rows, _ = w_hbm.shape
    wide, hw = wqkv.shape[1], wo.shape[2]
    n_col = n_dev // 2
    copies = []
    for i in range(n_dev):
        copies.append(pltpu.make_async_copy(w_hbm.at[i, :, pl.ds(0, wide)], wqkv.at[pl.ds(i * rows, rows), :], sem))
        for j in range(2):
            dst = wo.at[i // n_col, pl.ds((i % n_col * 2 + j) * rows, rows), :]
            copies.append(pltpu.make_async_copy(w_hbm.at[i, :, pl.ds(wide + j * hw, hw)], dst, sem))
    for cp in copies:
        cp.start()
    for cp in copies:
        cp.wait()


def inv_rms_of(wide_vals):
    return lax.rsqrt(jnp.mean(wide_vals * wide_vals, axis=-1, keepdims=True) + 1e-6)


def head_lanes(shape, axis, head):
    lane = lax.broadcasted_iota(jnp.int32, shape, axis)
    return lane < 64 if head == 0 else lane >= 64


def causal_tail(values, fill):
    n, k = values.shape
    tail = values[:, k - n :]
    keep = lax.broadcasted_iota(jnp.int32, (n, n), 0) >= lax.broadcasted_iota(jnp.int32, (n, n), 1)
    tail = jnp.where(keep, tail, fill)
    return tail if k == n else jnp.concatenate([values[:, : k - n], tail], axis=1)


def attn_fwd_kernel(pos_ref, w_hbm, x_ref, h_ref, u_ref, qkv_ref, ctx_ref, lse_ref, pack_ref, wqkv, wo, acc, sem):
    i = pl.program_id(0)
    width = x_ref.shape[1]
    hw = width // 2
    seq = x_ref.shape[0]

    @pl.when(i == 0)
    def _():
        load_attention_weights(w_hbm, wqkv, wo, sem)

    x = x_ref[...].astype(F32)
    normed = (x * inv_rms_of(x)).astype(BF16)
    for t in range(3):
        cols = slice(t * width, (t + 1) * width)
        qkv_ref[:, cols] = mm(normed, wqkv[:, cols]).astype(BF16)
    for pair in range(width // 128):
        lanes = slice(pair * 128, (pair + 1) * 128)
        q = qkv_ref[:, lanes] * jnp.asarray(0.125, BF16)
        k = qkv_ref[:, width + pair * 128 : width + (pair + 1) * 128]
        v = qkv_ref[:, 2 * width + pair * 128 : 2 * width + (pair + 1) * 128]
        for j in range(seq // QUERY_BLOCK):
            rows = slice(j * QUERY_BLOCK, (j + 1) * QUERY_BLOCK)
            keys = slice(0, (j + 1) * QUERY_BLOCK)
            outs = []
            for head in range(2):
                qm = jnp.where(head_lanes((QUERY_BLOCK, 128), 1, head), q[rows], jnp.zeros((), BF16))
                s = causal_tail(mm(qm, k[keys], NT), -1e30)
                top = jnp.max(s, axis=1, keepdims=True)
                e = jnp.exp(s - top)
                total = jnp.sum(e, axis=1, keepdims=True)
                outs.append(mm((e * (1.0 / total)).astype(BF16), v[keys]))
                lse_ref[rows, pair * 2 + head : pair * 2 + head + 1] = top + jnp.log(total)
            ctx_ref[rows, lanes] = jnp.where(head_lanes((QUERY_BLOCK, 128), 1, 0), outs[0], outs[1]).astype(BF16)
    ctx = ctx_ref[...]
    for f in range(2):
        cols = slice(f * hw, (f + 1) * hw)
        h_ref[:, cols] = (x_ref[:, cols].astype(F32) + mm(ctx, wo[f])).astype(BF16)
    h = h_ref[...].astype(F32)
    u = (h * inv_rms_of(h)).astype(BF16)
    u_ref[...] = u
    hit = lax.broadcasted_iota(jnp.int32, (CHUNK, seq), 0) == pos_ref[pl.ds(i, 1), :]
    part = mm(jnp.where(hit, 1.0, 0.0).astype(BF16), u)

    @pl.when(i == 0)
    def _():
        acc[...] = part

    @pl.when(i > 0)
    def _():
        acc[...] += part

    @pl.when(i == pl.num_programs(0) - 1)
    def _():
        pack_ref[...] = acc[...].astype(BF16)


def attn_fwd(pos, w_all, x, n_seq):
    n, width = x.shape
    seq = n // n_seq
    rows = pl.BlockSpec((seq, width), lambda i: (i, 0))
    return pl.pallas_call(
        attn_fwd_kernel,
        grid=(n_seq,),
        out_shape=(
            jax.ShapeDtypeStruct((n, width), BF16),
            jax.ShapeDtypeStruct((n, width), BF16),
            jax.ShapeDtypeStruct((n, 3 * width), BF16),
            jax.ShapeDtypeStruct((n, width), BF16),
            jax.ShapeDtypeStruct((n, 128), F32),
            jax.ShapeDtypeStruct((CHUNK, width), BF16),
        ),
        in_specs=[pl.BlockSpec((n_seq, seq), lambda i: (0, 0)), ANY, rows],
        out_specs=(rows, rows, pl.BlockSpec((seq, 3 * width), lambda i: (i, 0)), rows, pl.BlockSpec((seq, 128), lambda i: (i, 0)), pl.BlockSpec((CHUNK, width), lambda i: (0, 0))),
        scratch_shapes=[pltpu.VMEM((width, 3 * width), BF16), pltpu.VMEM((2, width, width // 2), BF16), pltpu.VMEM((CHUNK, width), F32), pltpu.SemaphoreType.DMA],
        compiler_params=params(),
        cost_estimate=pl.CostEstimate(flops=30 * 10**9, bytes_accessed=50 * 2**20, transcendentals=0),
        name='attn_fwd',
    )(pos.reshape(n_seq, seq), w_all, x)


def norm_back(grad, wide_vals):
    inv = inv_rms_of(wide_vals)
    return inv * (grad - wide_vals * (inv * inv * jnp.mean(grad * wide_vals, axis=-1, keepdims=True)))


def attn_bwd_kernel(n_ref, pos_ref, first_ref, more_hbm, w_hbm, x_ref, h_ref, dout_ref, qkv_ref, ctx_ref, lse_ref, dx_ref, wqkv, wo, dqkv, dctx, dh, buf, sem):
    i = pl.program_id(0)
    seq, width = x_ref.shape
    hw = width // 2

    @pl.when(i == 0)
    def _():
        load_attention_weights(w_hbm, wqkv, wo, sem)

    pos = pos_ref[pl.ds(i, 1), :]
    row = lax.broadcasted_iota(jnp.int32, (CHUNK, seq), 0)

    def gathered(base, rows):
        return mm(jnp.where(row + base == pos, 1.0, 0.0).astype(BF16), rows, TN)

    dh[...] = gathered(0, first_ref[...])

    def more(c, carry):
        copy = pltpu.make_async_copy(more_hbm.at[c - 1], buf, sem)
        copy.start()
        copy.wait()
        dh[...] += gathered(c * CHUNK, buf[...])
        return carry

    lax.fori_loop(1, n_ref[0], more, 0)
    dh[...] = dout_ref[...].astype(F32) + norm_back(dh[...], h_ref[...].astype(F32))
    dh_b = dh[...].astype(BF16)
    dctx[...] = (mm(dh_b[:, :hw], wo[0], NT) + mm(dh_b[:, hw:], wo[1], NT)).astype(BF16)
    zero = jnp.zeros((), BF16)
    for pair in range(width // 128):
        lanes = slice(pair * 128, (pair + 1) * 128)
        k_lanes = slice(width + pair * 128, width + (pair + 1) * 128)
        v_lanes = slice(2 * width + pair * 128, 2 * width + (pair + 1) * 128)
        q = qkv_ref[:, lanes] * jnp.asarray(0.125, BF16)
        k, v = qkv_ref[:, k_lanes], qkv_ref[:, v_lanes]
        do = dctx[:, lanes]
        q_t, do_t = q.T, do.T
        prod = do.astype(F32) * ctx_ref[:, lanes].astype(F32)
        dk_t = [jnp.zeros((128, QUERY_BLOCK), F32) for _ in range(seq // QUERY_BLOCK)]
        dv_t = list(dk_t)
        for j in range(seq // QUERY_BLOCK):
            rows = slice(j * QUERY_BLOCK, (j + 1) * QUERY_BLOCK)
            keys = slice(0, (j + 1) * QUERY_BLOCK)
            dqs = []
            for head in range(2):
                mine = head_lanes((QUERY_BLOCK, 128), 1, head)
                mine_t = head_lanes((128, QUERY_BLOCK), 0, head)
                qm, dom = jnp.where(mine, q[rows], zero), jnp.where(mine, do[rows], zero)
                delta = jnp.sum(jnp.where(mine, prod[rows], 0.0), axis=1, keepdims=True)
                lse = lse_ref[rows, pair * 2 + head : pair * 2 + head + 1]
                p = jnp.exp(causal_tail(mm(qm, k[keys], NT) - lse, -1e30))
                dp = mm(dom, v[keys], NT)
                ds = (p * (dp - delta)).astype(BF16)
                pb = p.astype(BF16)
                dqs.append(mm(ds, k[keys]))
                qm_t, dom_t = jnp.where(mine_t, q_t[:, rows], zero), jnp.where(mine_t, do_t[:, rows], zero)
                dk_part, dv_part = mm(qm_t, ds), mm(dom_t, pb)
                for c in range(j + 1):
                    cols = slice(c * QUERY_BLOCK, (c + 1) * QUERY_BLOCK)
                    dk_t[c] = dk_t[c] + dk_part[:, cols]
                    dv_t[c] = dv_t[c] + dv_part[:, cols]
            dqkv[rows, lanes] = (jnp.where(head_lanes((QUERY_BLOCK, 128), 1, 0), dqs[0], dqs[1]) * 0.125).astype(BF16)
        for c in range(seq // QUERY_BLOCK):
            rows = slice(c * QUERY_BLOCK, (c + 1) * QUERY_BLOCK)
            dqkv[rows, k_lanes] = dk_t[c].astype(BF16).T
            dqkv[rows, v_lanes] = dv_t[c].astype(BF16).T
    dn = mm(dqkv[...], wqkv[...], NT)
    dx_ref[...] = (dh[...] + norm_back(dn, x_ref[...].astype(F32))).astype(BF16)


def attn_bwd(n_chunks, pos, first, more, w_all, x, h, dout, qkv, ctx, lse, n_seq):
    n, width = x.shape
    seq = n // n_seq
    rows = pl.BlockSpec((seq, width), lambda i: (i, 0))
    return pl.pallas_call(
        attn_bwd_kernel,
        grid=(n_seq,),
        out_shape=jax.ShapeDtypeStruct((n, width), BF16),
        in_specs=[SMEM, pl.BlockSpec((n_seq, seq), lambda i: (0, 0)), pl.BlockSpec((CHUNK, width), lambda i: (0, 0)), ANY, ANY, rows, rows, rows, pl.BlockSpec((seq, 3 * width), lambda i: (i, 0)), rows, pl.BlockSpec((seq, 128), lambda i: (i, 0))],
        out_specs=rows,
        scratch_shapes=[
            pltpu.VMEM((width, 3 * width), BF16),
            pltpu.VMEM((2, width, width // 2), BF16),
            pltpu.VMEM((seq, 3 * width), BF16),
            pltpu.VMEM((seq, width), BF16),
            pltpu.VMEM((seq, width), F32),
            pltpu.VMEM((CHUNK, width), BF16),
            pltpu.SemaphoreType.DMA,
        ],
        compiler_params=params(),
        cost_estimate=pl.CostEstimate(flops=50 * 10**9, bytes_accessed=60 * 2**20, transcendentals=0),
        name='attn_bwd',
    )(n_chunks.reshape(1), pos.reshape(n_seq, seq), first, more, w_all, x, h, dout, qkv, ctx, lse)


def experts_kernel(back, n_src, cnt_ref, prm_ref, u_hbm, dy_hbm, w1_hbm, w3_hbm, w2_hbm, r1_hbm, r3_hbm, r2_hbm, i1, i3, i2, *refs):
    if back:
        o1, o3, o2, y_hbm, du_hbm = refs[:5]
        scratch = refs[5:]
        y_acc, du_acc, stage, zero, row_sem = scratch[-5:]
        scratch = scratch[:-5]
    else:
        o1, o3, o2 = refs[:3]
        scratch = refs[3:]
    u_s, dy_s, ut_s, dyt_s, w1_s, w3_s, w2_s, d1_s, d3_s, d2_s, d2t_s, lst, load_sem, w_sem, d_sem = scratch
    expert, local, half, chunk, add_first = prm_ref[0], prm_ref[1], prm_ref[2], prm_ref[3], prm_ref[4]
    width = u_s.shape[1]
    hw = width // 2
    ff = w1_hbm.shape[2]
    n_ff = ff // FF_STEP
    first_tile = chunk * CHUNK_TILES
    own_rows = pl.ds(pl.multiple_of(half * hw, hw), hw)
    got_rows = pl.ds(pl.multiple_of((1 - half) * hw, hw), hw)

    if back:
        def unmark(t, carry):
            lst[1, t] = 0
            return carry

        lax.fori_loop(0, n_src * CHUNK_TILES, unmark, 0)
    total = jnp.int32(0)
    for s in range(n_src):
        off, own = jnp.int32(0), jnp.int32(0)
        for e in range(n_src):
            tiles = (cnt_ref[s, e] + (TILE - 1)) // TILE
            off = off + jnp.where(e < expert, tiles, 0)
            own = own + jnp.where(e == expert, tiles, 0)
        lo = jnp.clip(off - first_tile, 0, CHUNK_TILES)
        hi = jnp.clip(off + own - first_tile, 0, CHUNK_TILES)

        def note(j, t, s=s):
            lst[0, t] = s * CHUNK_TILES + j
            if back:
                lst[1, s * CHUNK_TILES + j] = 1
            return t + 1

        total = lax.fori_loop(lo, hi, note, total)

    def tile_of(ref, t):
        return ref.at[t // CHUNK_TILES, pl.ds(pl.multiple_of((t % CHUNK_TILES) * TILE, TILE), TILE), :]

    if back:
        zero[...] = jnp.zeros_like(zero)

        def clear(t, n):
            @pl.when(lst[1, t] == 0)
            def _():
                pltpu.make_async_copy(zero, tile_of(y_hbm, t), row_sem).start()
                pltpu.make_async_copy(zero, tile_of(du_hbm, t), row_sem).start()

            return n

        lax.fori_loop(0, n_src * CHUNK_TILES, clear, 0)

    def weights(f, slot):
        cols = pl.ds(pl.multiple_of(f * FF_STEP, FF_STEP), FF_STEP)
        pairs = [
            (w1_hbm.at[local, :, cols], w1_s.at[slot, own_rows, :]),
            (r1_hbm.at[:, cols], w1_s.at[slot, got_rows, :]),
            (w3_hbm.at[local, :, cols], w3_s.at[slot, own_rows, :]),
            (r3_hbm.at[:, cols], w3_s.at[slot, got_rows, :]),
            (w2_hbm.at[local, cols, :], w2_s.at[slot, :, own_rows]),
            (r2_hbm.at[cols, :], w2_s.at[slot, :, got_rows]),
        ]
        return [pltpu.make_async_copy(src, dst, w_sem.at[slot, i]) for i, (src, dst) in enumerate(pairs)]

    def grads(f, slot, ins):
        cols = pl.ds(pl.multiple_of(f * FF_STEP, FF_STEP), FF_STEP)
        hbm = (i1, i3, i2) if ins else (o1, o3, o2)
        pairs = [
            (hbm[0].at[local, :, cols], d1_s.at[slot]),
            (hbm[1].at[local, :, cols], d3_s.at[slot]),
            (hbm[2].at[local, cols, :], d2_s.at[slot]),
        ]
        if not ins:
            pairs = [(b, a) for a, b in pairs]
        return [pltpu.make_async_copy(src, dst, d_sem.at[slot, i]) for i, (src, dst) in enumerate(pairs)]

    def one_pass(p, carry):
        for cp in weights(0, 0):
            cp.start()
        n_tiles = jnp.clip(total - p * PASS_TILES, 0, PASS_TILES)
        n_blk = (n_tiles + (CHUNK_TILES - 1)) // CHUNK_TILES

        def rows_at(k):
            return pl.ds(pl.multiple_of(k * TILE, TILE), TILE)

        def load(k, carry):
            t = lst[0, p * PASS_TILES + k]
            pltpu.make_async_copy(tile_of(u_hbm, t), u_s.at[rows_at(k), :], load_sem).start()
            pltpu.make_async_copy(tile_of(dy_hbm, t), dy_s.at[rows_at(k), :], load_sem).start()
            return carry

        lax.fori_loop(0, n_tiles, load, 0)

        def fill(k, carry):
            u_s[rows_at(k), :] = jnp.zeros((TILE, width), BF16)
            dy_s[rows_at(k), :] = jnp.zeros((TILE, width), BF16)
            return carry

        lax.fori_loop(n_tiles, n_blk * CHUNK_TILES, fill, 0)

        def loaded(k, carry):
            pltpu.make_async_copy(tile_of(u_hbm, 0), u_s.at[rows_at(k), :], load_sem).wait()
            pltpu.make_async_copy(tile_of(dy_hbm, 0), dy_s.at[rows_at(k), :], load_sem).wait()
            return carry

        lax.fori_loop(0, n_tiles, loaded, 0)

        def flip(k, carry):
            ut_s[:, rows_at(k)] = u_s[rows_at(k), own_rows].T
            dyt_s[:, rows_at(k)] = dy_s[rows_at(k), own_rows].T
            return carry

        lax.fori_loop(0, n_blk * CHUNK_TILES, flip, 0)
        add = jnp.logical_or(p > 0, add_first > 0)

        def step(f, carry):
            slot = f % 2

            @pl.when(f + 1 < n_ff)
            def _():
                for cp in weights(f + 1, 1 - slot):
                    cp.start()

            @pl.when(f >= 2)
            def _():
                for cp in grads(f - 2, slot, False):
                    cp.wait()

            for cp in weights(f, slot):
                cp.wait()

            d1_s[slot] = jnp.zeros((hw, FF_STEP), F32)
            d3_s[slot] = jnp.zeros((hw, FF_STEP), F32)
            d2t_s[...] = jnp.zeros((hw, FF_STEP), F32)

            @pl.when(add)
            def _():
                for cp in grads(f, slot, True):
                    cp.start()
                for cp in grads(f, slot, True):
                    cp.wait()
                d2t_s[...] = d2_s[slot].T

            def block(b, carry):
                rows = pl.ds(pl.multiple_of(b * CHUNK, CHUNK), CHUNK)
                w1, w3, w2 = w1_s[slot], w3_s[slot], w2_s[slot]
                u, dy = u_s[rows, :], dy_s[rows, :]
                act_a = mm(u, w1)
                act_b = mm(u, w3)
                d_g = mm(dy, w2, NT)
                sig = 0.5 * jnp.tanh(0.5 * act_a) + 0.5
                silu = act_a * sig
                g = (silu * act_b).astype(BF16)
                d_b = (d_g * silu).astype(BF16)
                d_a = (d_g * act_b * (sig + silu * (1.0 - sig))).astype(BF16)
                if back:
                    y = mm(g, w2)
                    du = mm(d_a, w1, NT) + mm(d_b, w3, NT)

                    @pl.when(f == 0)
                    def _():
                        y_acc[rows, :] = y
                        du_acc[rows, :] = du

                    @pl.when(f > 0)
                    def _():
                        y_acc[rows, :] += y
                        du_acc[rows, :] += du

                d1_s[slot] += mm(ut_s[:, rows], d_a)
                d3_s[slot] += mm(ut_s[:, rows], d_b)
                d2t_s[...] += mm(dyt_s[:, rows], g)
                return carry

            lax.fori_loop(0, n_blk, block, 0)
            d2_s[slot] = d2t_s[...].T
            for cp in grads(f, slot, False):
                cp.start()
            return carry

        lax.fori_loop(0, n_ff, step, 0)
        if back:
            def put(k, carry):
                t = lst[0, p * PASS_TILES + k]
                stage[0, rows_at(k), :] = y_acc[rows_at(k), :].astype(BF16)
                stage[1, rows_at(k), :] = du_acc[rows_at(k), :].astype(BF16)
                pltpu.make_async_copy(stage.at[0, rows_at(k), :], tile_of(y_hbm, t), row_sem).start()
                pltpu.make_async_copy(stage.at[1, rows_at(k), :], tile_of(du_hbm, t), row_sem).start()
                return carry

            lax.fori_loop(0, n_tiles, put, 0)

            def done(k, carry):
                pltpu.make_async_copy(zero, tile_of(y_hbm, 0), row_sem).wait()
                pltpu.make_async_copy(zero, tile_of(du_hbm, 0), row_sem).wait()
                return carry

            lax.fori_loop(0, n_tiles, done, 0)
        for f in (n_ff - 2, n_ff - 1):
            for cp in grads(f, f % 2, False):
                cp.wait()
        return carry

    n_pass = jnp.maximum((total + (PASS_TILES - 1)) // PASS_TILES, 1)
    lax.fori_loop(0, n_pass, one_pass, 0)
    if back:
        def cleared(t, carry):
            pltpu.make_async_copy(zero, tile_of(y_hbm, 0), row_sem).wait()
            pltpu.make_async_copy(zero, tile_of(du_hbm, 0), row_sem).wait()
            return carry

        lax.fori_loop(0, n_src * CHUNK_TILES - total, cleared, 0)


def experts(back, counts, prm, u_all, dy_all, own, got, dws):
    n_src, _, width = u_all.shape
    hw = width // 2
    ff = own[0].shape[2]
    rows = PASS_TILES * TILE
    scratch = [
        pltpu.VMEM((rows, width), BF16),
        pltpu.VMEM((rows, width), BF16),
        pltpu.VMEM((hw, rows), BF16),
        pltpu.VMEM((hw, rows), BF16),
        pltpu.VMEM((2, width, FF_STEP), BF16),
        pltpu.VMEM((2, width, FF_STEP), BF16),
        pltpu.VMEM((2, FF_STEP, width), BF16),
        pltpu.VMEM((2, hw, FF_STEP), F32),
        pltpu.VMEM((2, hw, FF_STEP), F32),
        pltpu.VMEM((2, FF_STEP, hw), F32),
        pltpu.VMEM((hw, FF_STEP), F32),
        pltpu.SMEM((2, n_src * CHUNK_TILES), jnp.int32),
        pltpu.SemaphoreType.DMA,
        pltpu.SemaphoreType.DMA((2, 6)),
        pltpu.SemaphoreType.DMA((2, 3)),
    ]
    outs = [jax.ShapeDtypeStruct(d.shape, d.dtype) for d in dws]
    if back:
        outs += [jax.ShapeDtypeStruct(u_all.shape, BF16)] * 2
        scratch += [
            pltpu.VMEM((rows, width), F32),
            pltpu.VMEM((rows, width), F32),
            pltpu.VMEM((2, rows, width), BF16),
            pltpu.VMEM((TILE, width), BF16),
            pltpu.SemaphoreType.DMA,
        ]
    units = 7.5 if back else 4.5
    return pl.pallas_call(
        functools.partial(experts_kernel, back, n_src),
        out_shape=tuple(outs),
        in_specs=[SMEM, SMEM] + [ANY] * 11,
        out_specs=tuple([ANY] * len(outs)),
        scratch_shapes=scratch,
        input_output_aliases={10: 0, 11: 1, 12: 2},
        compiler_params=params(),
        cost_estimate=pl.CostEstimate(flops=int(units * 2 * 2 * CHUNK * width * ff), bytes_accessed=30 * 2**20, transcendentals=0),
        name='experts_back' if back else 'experts_grad',
    )(counts, prm, u_all, dy_all, *own, *got, *dws)


def unset_kernel(*refs):
    pass


def unset(*shapes):
    outs = tuple(jax.ShapeDtypeStruct(s, d) for s, d in shapes)
    return pl.pallas_call(unset_kernel, out_shape=outs, out_specs=tuple([ANY] * len(outs)), name='unset')()


def solution(mesh):
    n_dev = mesh.shape['fsdp'] * mesh.shape['ep']
    tok_spec = P(('data', 'fsdp', 'ep'))
    in_specs = (tok_spec, P('fsdp'), P(None, None, 'fsdp'), P('ep', 'fsdp'), P('ep', 'fsdp'), P('ep', None, 'fsdp'), tok_spec, tok_spec, tok_spec, tok_spec)
    out_specs = (tok_spec, tok_spec, P(('data', 'ep'), 'fsdp'), P(('data', 'ep'), 'fsdp'), P(('data', 'ep'), None, 'fsdp'))

    def device_fn(tokens, w_qkv, w_out, w_gate, w_up, w_down, expert_idx, expert_slot, gate_wts, d_out):
        n_seq, seq_len, d_model = tokens.shape
        n_tok = n_seq * seq_len
        n_exp = n_dev
        half = lax.axis_index('fsdp').astype(jnp.int32)
        col = lax.axis_index('ep').astype(jnp.int32)
        swap = [(0, 1), (1, 0)]
        own = (w_gate, w_up, w_down)

        def other(local):
            got = []
            for w in own:
                piece = lax.dynamic_index_in_dim(w, local, 0, keepdims=False)
                got.append(lax.ppermute(piece, 'fsdp', swap))
            return got

        n_col = mesh.shape['ep']
        hw = w_qkv.shape[0]
        eighth = hw // n_col
        qkv_part = lax.dynamic_slice_in_dim(w_qkv.reshape(hw, 3 * d_model), col * eighth, eighth, 0)
        out_part = lax.dynamic_slice_in_dim(w_out.reshape(d_model, hw), col * 2 * eighth, 2 * eighth, 0)
        w_part = jnp.concatenate([qkv_part, out_part[:eighth], out_part[eighth:]], axis=1)
        w_all = lax.all_gather(w_part, GROUP)
        x_tok = tokens.reshape(n_tok, d_model)
        pos, cnt = route(expert_idx, expert_slot, n_exp)
        counts = lax.all_gather(cnt[0], GROUP)
        got_mine = other(1 - half)
        gate = gate_wts.reshape(n_tok // PACK_STEP, PACK_STEP).astype(F32)
        dout_tok = d_out.reshape(n_tok, d_model)
        zero = jnp.int32(0)
        dy_all = lax.all_gather(pack(zero, counts, pos, gate, dout_tok, True), GROUP)
        got_rest = other(half)

        h_tok, u_tok, qkv, ctx, lse, u_pack = attn_fwd(pos, w_all, x_tok, n_seq)
        u_all = lax.all_gather(u_pack, GROUP)

        tiles = (counts[:, :n_exp] + (TILE - 1)) // TILE
        n_chunks = jnp.max((jnp.sum(tiles, axis=1) + (CHUNK_TILES - 1)) // CHUNK_TILES)
        max_more = (n_tok + n_exp * (TILE - 1)) // CHUNK

        def prm(local, chunk, add):
            return jnp.stack([2 * col + local, local, half, chunk, add]).astype(jnp.int32)

        dws = unset(*[(w.shape, F32) for w in own])
        more_y, more_du = unset(*[((max_more, CHUNK, d_model), BF16)] * 2)
        *dws, y_all, du_all = experts(True, counts, prm(half, zero, zero), u_all, dy_all, own, got_mine, dws)
        first_du = lax.psum_scatter(du_all, GROUP, scatter_dimension=0)
        first_y = lax.psum_scatter(y_all, GROUP, scatter_dimension=0)

        def fetch(c):
            return lax.all_gather(pack(c, counts, pos, gate, u_tok, False), GROUP), lax.all_gather(pack(c, counts, pos, gate, dout_tok, True), GROUP)

        def more_back(state):
            c, d1, d3, d2, ys, dus = state
            u_c, dy_c = fetch(c)
            d1, d3, d2, y_c, du_c = experts(True, counts, prm(half, c, jnp.int32(1)), u_c, dy_c, own, got_mine, (d1, d3, d2))
            y_c = lax.psum_scatter(y_c, GROUP, scatter_dimension=0)
            du_c = lax.psum_scatter(du_c, GROUP, scatter_dimension=0)
            ys = lax.dynamic_update_index_in_dim(ys, y_c, c - 1, 0)
            dus = lax.dynamic_update_index_in_dim(dus, du_c, c - 1, 0)
            return c + 1, d1, d3, d2, ys, dus

        def more_grad(state):
            c, d1, d3, d2 = state
            u_c, dy_c = fetch(c)
            d1, d3, d2 = experts(False, counts, prm(1 - half, c, jnp.int32(1)), u_c, dy_c, own, got_rest, (d1, d3, d2))
            return c + 1, d1, d3, d2

        _, *dws, more_y, more_du = lax.while_loop(lambda s: s[0] < n_chunks, more_back, (jnp.int32(1), *dws, more_y, more_du))
        layer_out = unpack(n_chunks, pos, gate, h_tok, first_y, more_y).reshape(n_seq, seq_len, d_model)
        d_tokens = attn_bwd(n_chunks, pos, first_du, more_du, w_all, x_tok, h_tok, dout_tok, qkv, ctx, lse, n_seq).reshape(n_seq, seq_len, d_model)

        dws = experts(False, counts, prm(1 - half, zero, zero), u_all, dy_all, own, got_rest, dws)
        _, *dws = lax.while_loop(lambda s: s[0] < n_chunks, more_grad, (jnp.int32(1), *dws))
        return layer_out, d_tokens, *dws

    return jax.shard_map(device_fn, mesh=mesh, in_specs=in_specs, out_specs=out_specs, check_vma=False)
```

profile of v0, /device:TPU:0, one launch (start us, length us, event | category | flops | bytes accessed | tf_op | source)
XLA Modules:
  0.0 818.0 jit_solution(5260119024993925501)
XLA Ops:
  7.2 0.0 copy-start
  7.2 0.0 all-gather.28.cloned.1.call-start
  7.2 1.4 copy-done
  8.6 0.2 constant_dynamic-slice_fusion.2
  8.9 0.2 copy.30
  9.1 0.9 constant_dynamic-slice_fusion
  10.1 0.9 pad_maximum_fusion
  11.0 0.0 all-gather.28.cloned.1.call-update
  11.0 0.0 all-gather.32.cloned.1.call-start
  11.0 0.7 reshape.77.gate_ref
  11.7 2.4 route.1
  14.1 0.6 reshape.72.pos_ref
  14.7 12.1 %all-gather.7 = s32[8,1,128]{2,1,0:T(1,128)S(1)} all-gather(s32[1,1,128]{2,1,0:T(1,128)} %bitcast.94), channel_id=1, replica_groups=mesh['data'=1,'fsdp'=2,'ep'=4] {'fsdp','ep'}, dimensions={0}, use_global_device_ids=true | all-gather | bytes 4608 | tf_op jit(solution)/shard_map/all_gather | solution.py:687
  26.8 8.1 pack.21
  34.9 0.0 all-gather.32.cloned.1.call-update
  35.0 0.5 all-gather.30.cloned.1.call-start
  35.5 0.6 reshape.68.pos_ref
  36.1 11.1 %all-gather.28.cloned.1.call-done = bf16[768,3072]{1,0:T(8,128)(2,1)} async-done(((bf16[96,3072]{1,0:T(8,128)(2,1)}), bf16[768,3072]{1,0:T(8,128)(2,1)}) %all-gather.28.cloned.1.call-update) | async-done | bytes 4718608 | tf_op jit(solution)/shard_map/all_gather | solution.py:684
  47.2 104.8 %attn_fwd.1 = (bf16[4096,768]{1,0:T(8,128)(2,1)}, bf16[4096,768]{1,0:T(8,128)(2,1)}, bf16[4096,2304]{1,0:T(8,128)(2,1)}, bf16[4096,768]{1,0:T(8,128)(2,1)}, f32[...) custom-call(s32[8,512]{1,0:T(8,128)} %reshape.68.pos_ref, bf16[8,96,3072]{2,1,0:T(8,128)(2,1)} %bitcast.107, ...), custom_call_target="tpu_custom_call" | custom-call | flops 30000001024 | bytes 52428800 | tf_op jit(solution)/shard_map/attn_fwd/pallas_call | solution.py:260
  152.0 0.0 slice-start
  152.0 0.0 all-gather.30.cloned.1.call-update
  152.0 0.0 slice-start.1
  152.0 5.0 dynamic-slice_bitcast_fusion.2
  157.1 1.3 collective-permute-start
  158.3 0.0 slice-done
  158.3 0.0 slice-done.1
  158.3 2.5 dynamic-slice_bitcast_fusion.1
  160.8 0.9 collective-permute-start.1
  161.7 0.0 slice-done.2
  161.7 0.0 slice-done.3
  161.7 2.6 dynamic-slice_bitcast_fusion
  164.3 1.1 collective-permute-start.2
  165.4 0.0 copy-done.2
  165.5 0.7 pad_add_fusion
  166.1 0.1 fusion.1
  166.2 0.7 fusion.3
  166.9 75.8 %collective-permute-done.r1_hbm = bf16[384,3072]{1,0:T(8,128)(2,1)} collective-permute-done((bf16[384,3072]{1,0:T(8,128)(2,1)}, bf16[384,3072]{1,0:T(8,128)(2,1)}, u32[]{:S(2)}, u32[]{:S(2)}) %collective-permute-start) | collective-permute-done | bytes 2359328 | tf_op jit(solution)/shard_map/ppermute | solution.py:675
  242.7 50.6 %collective-permute-done.1.r3_hbm = bf16[384,3072]{1,0:T(8,128)(2,1)} collective-permute-done((bf16[384,3072]{1,0:T(8,128)(2,1)}, bf16[384,3072]{1,0:T(8,128)(2,1)}, u32[]{:S(2)}, u32[]{:S(2)}) %collective-permute-start.1) | collective-permute-done | bytes 2359328 | tf_op jit(solution)/shard_map/ppermute | solution.py:675
  293.3 50.2 %collective-permute-done.2.r2_hbm = bf16[3072,384]{1,0:T(8,128)(2,1)} collective-permute-done((bf16[3072,384]{1,0:T(8,128)(2,1)}, bf16[3072,384]{1,0:T(8,128)(2,1)}, u32[]{:S(2)}, u32[]{:S(2)}) %collective-permute-start.2) | collective-permute-done | bytes 2359328 | tf_op jit(solution)/shard_map/ppermute | solution.py:675
  343.5 44.5 %experts_back.8 = (f32[2,384,3072]{2,1,0:T(8,128)}, f32[2,384,3072]{2,1,0:T(8,128)}, f32[2,3072,384]{2,1,0:T(8,128)}, bf16[8,640,768]{2,1,0:T(8,128)(2,1)}, bf16[8,640,768]{2,1,0:T(8,128)(2,1)}) custom-call(s32[8,128]{1,0:T(8,128)S(1)} %bitcast.90, s32[5]{0:T(128)} %get-tuple-element.756.prm_ref, ...), custom_call_target="tpu_custom_call", output_to_operand_aliasing={{0}: (10, {}), {1}: (11, {}), {2}: (12, {})} | custom-call | flops 45298483200 | bytes 31457280 | tf_op jit(solution)/shard_map/experts_back/pallas_call | solution.py:634
  388.0 0.6 while.40
  388.7 0.0 reduce-scatter.5.cloned.1.call-start
  388.7 0.0 copy-start.3
  388.7 0.0 copy-start.4
  388.7 0.5 reduce-scatter.5.cloned.1.call-update
  389.2 0.0 reduce-scatter.7.cloned.1.call-start
  389.3 0.5 reduce-scatter.7.cloned.1.call-update
  389.8 34.4 %collective-permute-start.3 = (bf16[384,3072]{1,0:T(8,128)(2,1)}, bf16[384,3072]{1,0:T(8,128)(2,1)}, u32[]{:S(2)}, u32[]{:S(2)}) collective-permute-start(bf16[384,3072]{1,0:T(8,128)(2,1)} %get-tuple-element.751), channel_id=1, source_target_pairs={{0,4},{4,0},{1,5},{5,1},{2,6},{6,2},{3,7},{7,3}} | collective-permute-start | bytes 7077896 | tf_op jit(solution)/shard_map/ppermute | solution.py:675
  424.2 0.0 collective-permute-start.4
  424.3 2.0 collective-permute-start.5
  426.3 0.0 copy-done.3
  426.3 0.0 copy-done.4
  426.3 0.6 convert_bitcast_fusion.gate_ref
  426.9 73.9 %collective-permute-done.3.r1_hbm = bf16[384,3072]{1,0:T(8,128)(2,1)} collective-permute-done((bf16[384,3072]{1,0:T(8,128)(2,1)}, bf16[384,3072]{1,0:T(8,128)(2,1)}, u32[]{:S(2)}, u32[]{:S(2)}) %collective-permute-start.3) | collective-permute-done | bytes 2359328 | tf_op jit(solution)/shard_map/ppermute | solution.py:675
  500.8 74.8 %collective-permute-done.4.r3_hbm = bf16[384,3072]{1,0:T(8,128)(2,1)} collective-permute-done((bf16[384,3072]{1,0:T(8,128)(2,1)}, bf16[384,3072]{1,0:T(8,128)(2,1)}, u32[]{:S(2)}, u32[]{:S(2)}) %collective-permute-start.4) | collective-permute-done | bytes 2359328 | tf_op jit(solution)/shard_map/ppermute | solution.py:675
  575.6 64.5 %collective-permute-done.5.r2_hbm = bf16[3072,384]{1,0:T(8,128)(2,1)} collective-permute-done((bf16[3072,384]{1,0:T(8,128)(2,1)}, bf16[3072,384]{1,0:T(8,128)(2,1)}, u32[]{:S(2)}, u32[]{:S(2)}) %collective-permute-start.5) | collective-permute-done | bytes 2359328 | tf_op jit(solution)/shard_map/ppermute | solution.py:675
  640.1 43.3 %experts_grad.4 = (f32[2,384,3072]{2,1,0:T(8,128)}, f32[2,384,3072]{2,1,0:T(8,128)}, f32[2,3072,384]{2,1,0:T(8,128)}) custom-call(s32[8,128]{1,0:T(8,128)S(1)} %get-tuple-element.1377, s32[5]{0:T(128)} %get-tuple-element.755.prm_ref, bf16[8,640,768]{2,1,0:T(8,128)(2,1)} %bitcast.98, ...), custom_call_target="tpu_custom_call", output_to_operand_aliasing={{0}: (10, {}), {1}: (11, {}), {2}: (12, {})} | custom-call | flops 27179089920 | bytes 31457280 | tf_op jit(solution)/shard_map/experts_grad/pallas_call | solution.py:634
  683.4 0.0 reduce-scatter.5.cloned.1.call-done
  683.5 12.3 %unpack.1 = bf16[4096,768]{1,0:T(8,128)(2,1)} custom-call(s32[1]{0:T(128)} %bitcast.15.n_ref, s32[8,512]{1,0:T(8,128)} %reshape.68.pos_ref, f32[8,512]{1,0:T(8,128)} %convert_bitcast_fusion.gate_ref, bf16[4096,768]{1,0:T(8,128)(2,1)} %get-tuple-element.642.refs_0_.h_ref, bf16[640,768]{1,0:T(8,128)(2,1)} %bitcast.86, ...), custom_call_target="tpu_custom_call" | custom-call | flops 4026531840 | bytes 12582912 | tf_op jit(solution)/shard_map/unpack/pallas_call | solution.py:151
  695.8 0.0 reduce-scatter.7.cloned.1.call-done
  695.8 113.3 %attn_bwd.1 = bf16[4096,768]{1,0:T(8,128)(2,1)} custom-call(s32[1]{0:T(128)} %bitcast.15.n_ref, s32[8,512]{1,0:T(8,128)} %reshape.68.pos_ref, bf16[640,768]{1,0:T(8,128)(2,1)} %bitcast.109, bf16[7,640,768]{2,1,0:T(8,128)(2,1)} %get-tuple-element.656.more_hbm, bf16[8,96,3072]{2,1,0:T(8,128)(2,1)} %bitcast.108, bf16[4096,768]{1,0:T(8,128)(2,1)} %bitcast.104, ...), custom_call_target="tpu_custom_call" | custom-call | flops 49999998976 | bytes 62914560 | tf_op jit(solution)/shard_map/attn_bwd/pallas_call | solution.py:359
  809.2 0.6 while.41
  809.8 0.0 copy-start.1
  809.8 1.5 copy-done.1
  (12 shorter events, 0.0 us)
Async XLA Ops:
  7.2 1.5 copy-start
  7.2 40.0 %all-gather.28.cloned.1.call-start = ((), (), s32[]{:S(2)}) async-start(), calls=%async_computation.6 | async-start | bytes 5308416 | tf_op jit(solution)/shard_map/all_gather | solution.py:684
  11.0 332.5 %all-gather.32.cloned.1.call-start = ((), (), s32[]{:S(2)}) async-start(), calls=%async_computation.8 | async-start | bytes 8847360 | tf_op jit(solution)/shard_map/all_gather | solution.py:692
  14.1 151.3 %copy-start.2 = (s32[32,128]{1,0:T(8,128)}, s32[32,128]{1,0:T(8,128)S(1)}, u32[]{:S(2)}) copy-start(s32[32,128]{1,0:T(8,128)S(1)} %get-tuple-element.1275) | copy-start | bytes 49156
  35.0 308.5 %all-gather.30.cloned.1.call-start = ((), (), s32[]{:S(2)}) async-start(), calls=%async_computation.7 | async-start | bytes 8847360 | tf_op jit(solution)/shard_map/all_gather | solution.py:696
  152.0 6.4 slice-start
  152.0 6.3 slice-start.1
  157.1 4.7 slice-start.2
  157.1 4.7 slice-start.3
  157.1 85.7 %collective-permute-start = (bf16[384,3072]{1,0:T(8,128)(2,1)}, bf16[384,3072]{1,0:T(8,128)(2,1)}, u32[]{:S(2)}, u32[]{:S(2)}) collective-permute-start(bf16[384,3072]{1,0:T(8,128)(2,1)} %get-tuple-element.752), channel_id=1, source_target_pairs={{0,4},{4,0},{1,5},{5,1},{2,6},{6,2},{3,7},{7,3}} | collective-permute-start | bytes 7077896 | tf_op jit(solution)/shard_map/ppermute | solution.py:675
  160.8 132.5 %collective-permute-start.1 = (bf16[384,3072]{1,0:T(8,128)(2,1)}, bf16[384,3072]{1,0:T(8,128)(2,1)}, u32[]{:S(2)}, u32[]{:S(2)}) collective-permute-start(bf16[384,3072]{1,0:T(8,128)(2,1)} %get-tuple-element.750), channel_id=1, source_target_pairs={{0,4},{4,0},{1,5},{5,1},{2,6},{6,2},{3,7},{7,3}} | collective-permute-start | bytes 7077896 | tf_op jit(solution)/shard_map/ppermute | solution.py:675
  164.3 179.2 %collective-permute-start.2 = (bf16[3072,384]{1,0:T(8,128)(2,1)}, bf16[3072,384]{1,0:T(8,128)(2,1)}, u32[]{:S(2)}, u32[]{:S(2)}) collective-permute-start(bf16[3072,384]{1,0:T(8,128)(2,1)} %get-tuple-element.748), channel_id=1, source_target_pairs={{0,4},{4,0},{1,5},{5,1},{2,6},{6,2},{3,7},{7,3}} | collective-permute-start | bytes 7077896 | tf_op jit(solution)/shard_map/ppermute | solution.py:675
  388.7 294.8 %reduce-scatter.5.cloned.1.call-start = ((), (), s32[]{:S(2)}) async-start(), calls=%async_computation.4 | async-start | bytes 8847360 | tf_op jit(solution)/shard_map/reduce_scatter | solution.py:709
  388.7 37.6 %copy-start.3 = (s32[32,128]{1,0:T(8,128)S(1)}, s32[32,128]{1,0:T(8,128)}, u32[]{:S(2)}) copy-start(s32[32,128]{1,0:T(8,128)} %get-tuple-element.1375) | copy-start | bytes 49156
  388.7 37.6 %copy-start.4 = (bf16[8,512,1]{1,0,2:T(8,128)(2,1)S(1)}, bf16[8,512,1]{1,0,2:T(8,128)(2,1)}, u32[]{:S(2)}) copy-start(bf16[8,512,1]{1,0,2:T(8,128)(2,1)} %param.22) | copy-start | bytes 24580
  389.2 306.6 %reduce-scatter.7.cloned.1.call-start = ((), (), s32[]{:S(2)}) async-start(), calls=%async_computation.5 | async-start | bytes 8847360 | tf_op jit(solution)/shard_map/reduce_scatter | solution.py:708
  389.8 111.0 %collective-permute-start.3 = (bf16[384,3072]{1,0:T(8,128)(2,1)}, bf16[384,3072]{1,0:T(8,128)(2,1)}, u32[]{:S(2)}, u32[]{:S(2)}) collective-permute-start(bf16[384,3072]{1,0:T(8,128)(2,1)} %get-tuple-element.751), channel_id=1, source_target_pairs={{0,4},{4,0},{1,5},{5,1},{2,6},{6,2},{3,7},{7,3}} | collective-permute-start | bytes 7077896 | tf_op jit(solution)/shard_map/ppermute | solution.py:675
  424.2 151.3 %collective-permute-start.4 = (bf16[384,3072]{1,0:T(8,128)(2,1)}, bf16[384,3072]{1,0:T(8,128)(2,1)}, u32[]{:S(2)}, u32[]{:S(2)}) collective-permute-start(bf16[384,3072]{1,0:T(8,128)(2,1)} %get-tuple-element.749), channel_id=1, source_target_pairs={{0,4},{4,0},{1,5},{5,1},{2,6},{6,2},{3,7},{7,3}} | collective-permute-start | bytes 7077896 | tf_op jit(solution)/shard_map/ppermute | solution.py:675
  424.3 215.8 %collective-permute-start.5 = (bf16[3072,384]{1,0:T(8,128)(2,1)}, bf16[3072,384]{1,0:T(8,128)(2,1)}, u32[]{:S(2)}, u32[]{:S(2)}) collective-permute-start(bf16[3072,384]{1,0:T(8,128)(2,1)} %get-tuple-element.747), channel_id=1, source_target_pairs={{0,4},{4,0},{1,5},{5,1},{2,6},{6,2},{3,7},{7,3}} | collective-permute-start | bytes 7077896 | tf_op jit(solution)/shard_map/ppermute | solution.py:675
  809.8 1.5 copy-start.1
Sparse Core Ops, SparseCore 0:
  11.1 36.0 all-gather.27
  49.0 46.4 all-gather.31
  152.1 78.3 all-gather.29
  392.5 125.8 reduce-scatter.4
  521.7 92.8 reduce-scatter.6
where the time goes:
time: 821 us; the launch traced here: 818 us
  waiting for transfers between devices  402 us (49%)
  Pallas kernels  329 us (40%)
  starting transfers between devices  40.4 us (5%)
  local copies, waits for them, and re-layouts  16.4 us (2%)
  between operations  14.2 us (2%)
  blocking collectives  12.1 us (1%)
    ppermute x6, waiting for transfers between devices, other(): got.append(lax.ppermute(piece, 'fsdp', swap))  390 us
    pallas_call x1, Pallas kernels, attn_bwd(): pl.pallas_call(attn_bwd_kernel, grid=(n_seq,), out_shape=jax.ShapeDtypeSt...  113 us
    pallas_call x1, Pallas kernels, attn_fwd(): pl.pallas_call(attn_fwd_kernel, grid=(n_seq,), out_shape=(jax.ShapeDtypeS...  105 us
    pallas_call x2, Pallas kernels, experts(): pl.pallas_call(functools.partial(experts_kernel, back, n_src), out_shape=...  87.8 us
    ppermute x6, starting transfers between devices, other(): got.append(lax.ppermute(piece, 'fsdp', swap))  39.7 us
  transfers between devices with their start and end apart: 11, of which 7 were waited for; matrix products, arithmetic and copies ran while one was open for 2% of the time, Pallas kernels for 21%

commit v1 on v0

--- a/solution.py
+++ b/solution.py
@@ -15,6 +15,7 @@
 CHUNK = TILE * CHUNK_TILES
 PASS_TILES = 20
 FF_STEP = 512
+N_PARTS = 3
 GROUP = ('fsdp', 'ep')
 NN = (((1,), (0,)), ((), ()))
 NT = (((1,), (1,)), ((), ()))
@@ -197,7 +198,7 @@
     return tail if k == n else jnp.concatenate([values[:, : k - n], tail], axis=1)
 
 
-def attn_fwd_kernel(pos_ref, w_hbm, x_ref, h_ref, u_ref, qkv_ref, ctx_ref, lse_ref, pack_ref, wqkv, wo, acc, sem):
+def attn_fwd_kernel(pos_ref, w_hbm, x_ref, h_ref, u_ref, qkv_ref, ctx_ref, p0_ref, p1_ref, pack_ref, wqkv, wo, acc, sem):
     i = pl.program_id(0)
     width = x_ref.shape[1]
     hw = width // 2
@@ -227,8 +228,9 @@
                 top = jnp.max(s, axis=1, keepdims=True)
                 e = jnp.exp(s - top)
                 total = jnp.sum(e, axis=1, keepdims=True)
-                outs.append(mm((e * (1.0 / total)).astype(BF16), v[keys]))
-                lse_ref[rows, pair * 2 + head : pair * 2 + head + 1] = top + jnp.log(total)
+                p = (e * (1.0 / total)).astype(BF16)
+                (p0_ref, p1_ref)[j][0, pair * 2 + head] = p
+                outs.append(mm(p, v[keys]))
             ctx_ref[rows, lanes] = jnp.where(head_lanes((QUERY_BLOCK, 128), 1, 0), outs[0], outs[1]).astype(BF16)
     ctx = ctx_ref[...]
     for f in range(2):
@@ -251,6 +253,14 @@
     @pl.when(i == pl.num_programs(0) - 1)
     def _():
         pack_ref[...] = acc[...].astype(BF16)
+
+
+def probs_shapes(n_seq, width):
+    return [jax.ShapeDtypeStruct((n_seq, width // 64, QUERY_BLOCK, (j + 1) * QUERY_BLOCK), BF16) for j in range(2)]
+
+
+def probs_specs(width):
+    return [pl.BlockSpec((1, width // 64, QUERY_BLOCK, (j + 1) * QUERY_BLOCK), lambda i: (i, 0, 0, 0)) for j in range(2)]
 
 
 def attn_fwd(pos, w_all, x, n_seq):
@@ -265,11 +275,11 @@
             jax.ShapeDtypeStruct((n, width), BF16),
             jax.ShapeDtypeStruct((n, 3 * width), BF16),
             jax.ShapeDtypeStruct((n, width), BF16),
-            jax.ShapeDtypeStruct((n, 128), F32),
+            *probs_shapes(n_seq, width),
             jax.ShapeDtypeStruct((CHUNK, width), BF16),
         ),
         in_specs=[pl.BlockSpec((n_seq, seq), lambda i: (0, 0)), ANY, rows],
-        out_specs=(rows, rows, pl.BlockSpec((seq, 3 * width), lambda i: (i, 0)), rows, pl.BlockSpec((seq, 128), lambda i: (i, 0)), pl.BlockSpec((CHUNK, width), lambda i: (0, 0))),
+        out_specs=(rows, rows, pl.BlockSpec((seq, 3 * width), lambda i: (i, 0)), rows, *probs_specs(width), pl.BlockSpec((CHUNK, width), lambda i: (0, 0))),
         scratch_shapes=[pltpu.VMEM((width, 3 * width), BF16), pltpu.VMEM((2, width, width // 2), BF16), pltpu.VMEM((CHUNK, width), F32), pltpu.SemaphoreType.DMA],
         compiler_params=params(),
         cost_estimate=pl.CostEstimate(flops=30 * 10**9, bytes_accessed=50 * 2**20, transcendentals=0),
@@ -282,7 +292,7 @@
     return inv * (grad - wide_vals * (inv * inv * jnp.mean(grad * wide_vals, axis=-1, keepdims=True)))
 
 
-def attn_bwd_kernel(n_ref, pos_ref, first_ref, more_hbm, w_hbm, x_ref, h_ref, dout_ref, qkv_ref, ctx_ref, lse_ref, dx_ref, wqkv, wo, dqkv, dctx, dh, buf, sem):
+def attn_bwd_kernel(n_ref, pos_ref, first_ref, more_hbm, w_hbm, x_ref, h_ref, dout_ref, qkv_ref, ctx_ref, p0_ref, p1_ref, dx_ref, wqkv, wo, dqkv, dctx, dh, buf, sem):
     i = pl.program_id(0)
     seq, width = x_ref.shape
     hw = width // 2
@@ -329,13 +339,11 @@
             for head in range(2):
                 mine = head_lanes((QUERY_BLOCK, 128), 1, head)
                 mine_t = head_lanes((128, QUERY_BLOCK), 0, head)
-                qm, dom = jnp.where(mine, q[rows], zero), jnp.where(mine, do[rows], zero)
+                dom = jnp.where(mine, do[rows], zero)
                 delta = jnp.sum(jnp.where(mine, prod[rows], 0.0), axis=1, keepdims=True)
-                lse = lse_ref[rows, pair * 2 + head : pair * 2 + head + 1]
-                p = jnp.exp(causal_tail(mm(qm, k[keys], NT) - lse, -1e30))
+                pb = (p0_ref, p1_ref)[j][0, pair * 2 + head]
                 dp = mm(dom, v[keys], NT)
-                ds = (p * (dp - delta)).astype(BF16)
-                pb = p.astype(BF16)
+                ds = (pb.astype(F32) * (dp - delta)).astype(BF16)
                 dqs.append(mm(ds, k[keys]))
                 qm_t, dom_t = jnp.where(mine_t, q_t[:, rows], zero), jnp.where(mine_t, do_t[:, rows], zero)
                 dk_part, dv_part = mm(qm_t, ds), mm(dom_t, pb)
@@ -352,7 +360,7 @@
     dx_ref[...] = (dh[...] + norm_back(dn, x_ref[...].astype(F32))).astype(BF16)
 
 
-def attn_bwd(n_chunks, pos, first, more, w_all, x, h, dout, qkv, ctx, lse, n_seq):
+def attn_bwd(n_chunks, pos, first, more, w_all, x, h, dout, qkv, ctx, probs, n_seq):
     n, width = x.shape
     seq = n // n_seq
     rows = pl.BlockSpec((seq, width), lambda i: (i, 0))
@@ -360,7 +368,7 @@
         attn_bwd_kernel,
         grid=(n_seq,),
         out_shape=jax.ShapeDtypeStruct((n, width), BF16),
-        in_specs=[SMEM, pl.BlockSpec((n_seq, seq), lambda i: (0, 0)), pl.BlockSpec((CHUNK, width), lambda i: (0, 0)), ANY, ANY, rows, rows, rows, pl.BlockSpec((seq, 3 * width), lambda i: (i, 0)), rows, pl.BlockSpec((seq, 128), lambda i: (i, 0))],
+        in_specs=[SMEM, pl.BlockSpec((n_seq, seq), lambda i: (0, 0)), pl.BlockSpec((CHUNK, width), lambda i: (0, 0)), ANY, ANY, rows, rows, rows, pl.BlockSpec((seq, 3 * width), lambda i: (i, 0)), rows, *probs_specs(width)],
         out_specs=rows,
         scratch_shapes=[
             pltpu.VMEM((width, 3 * width), BF16),
@@ -374,15 +382,17 @@
         compiler_params=params(),
         cost_estimate=pl.CostEstimate(flops=50 * 10**9, bytes_accessed=60 * 2**20, transcendentals=0),
         name='attn_bwd',
-    )(n_chunks.reshape(1), pos.reshape(n_seq, seq), first, more, w_all, x, h, dout, qkv, ctx, lse)
-
-
-def experts_kernel(back, n_src, cnt_ref, prm_ref, u_hbm, dy_hbm, w1_hbm, w3_hbm, w2_hbm, r1_hbm, r3_hbm, r2_hbm, i1, i3, i2, *refs):
+    )(n_chunks.reshape(1), pos.reshape(n_seq, seq), first, more, w_all, x, h, dout, qkv, ctx, *probs)
+
+
+def experts_kernel(back, first, last, f_base, n_src, cnt_ref, prm_ref, u_hbm, dy_hbm, w1_hbm, w3_hbm, w2_hbm, r13_hbm, r2_hbm, i1, i3, i2, *refs):
     if back:
-        o1, o3, o2, y_hbm, du_hbm = refs[:5]
-        scratch = refs[5:]
-        y_acc, du_acc, stage, zero, row_sem = scratch[-5:]
-        scratch = scratch[:-5]
+        o1, o3, o2, y_part, du_part = refs[2:7]
+        scratch = refs[7:]
+        if last:
+            (y_hbm, du_hbm), scratch = scratch[:2], scratch[2:]
+        y_acc, du_acc, stage, zero, row_sem, part_sem = scratch[-6:]
+        scratch = scratch[:-6]
     else:
         o1, o3, o2 = refs[:3]
         scratch = refs[3:]
@@ -390,13 +400,12 @@
     expert, local, half, chunk, add_first = prm_ref[0], prm_ref[1], prm_ref[2], prm_ref[3], prm_ref[4]
     width = u_s.shape[1]
     hw = width // 2
-    ff = w1_hbm.shape[2]
-    n_ff = ff // FF_STEP
+    n_ff = r2_hbm.shape[0] // FF_STEP
     first_tile = chunk * CHUNK_TILES
     own_rows = pl.ds(pl.multiple_of(half * hw, hw), hw)
     got_rows = pl.ds(pl.multiple_of((1 - half) * hw, hw), hw)
 
-    if back:
+    if back and last:
         def unmark(t, carry):
             lst[1, t] = 0
             return carry
@@ -414,7 +423,7 @@
 
         def note(j, t, s=s):
             lst[0, t] = s * CHUNK_TILES + j
-            if back:
+            if back and last:
                 lst[1, s * CHUNK_TILES + j] = 1
             return t + 1
 
@@ -423,7 +432,7 @@
     def tile_of(ref, t):
         return ref.at[t // CHUNK_TILES, pl.ds(pl.multiple_of((t % CHUNK_TILES) * TILE, TILE), TILE), :]
 
-    if back:
+    if back and last:
         zero[...] = jnp.zeros_like(zero)
 
         def clear(t, n):
@@ -437,19 +446,20 @@
         lax.fori_loop(0, n_src * CHUNK_TILES, clear, 0)
 
     def weights(f, slot):
-        cols = pl.ds(pl.multiple_of(f * FF_STEP, FF_STEP), FF_STEP)
+        cols = pl.ds(pl.multiple_of(f_base + f * FF_STEP, FF_STEP), FF_STEP)
+        part = pl.ds(pl.multiple_of(f * FF_STEP, FF_STEP), FF_STEP)
         pairs = [
             (w1_hbm.at[local, :, cols], w1_s.at[slot, own_rows, :]),
-            (r1_hbm.at[:, cols], w1_s.at[slot, got_rows, :]),
+            (r13_hbm.at[pl.ds(0, hw), part], w1_s.at[slot, got_rows, :]),
             (w3_hbm.at[local, :, cols], w3_s.at[slot, own_rows, :]),
-            (r3_hbm.at[:, cols], w3_s.at[slot, got_rows, :]),
+            (r13_hbm.at[pl.ds(hw, hw), part], w3_s.at[slot, got_rows, :]),
             (w2_hbm.at[local, cols, :], w2_s.at[slot, :, own_rows]),
-            (r2_hbm.at[cols, :], w2_s.at[slot, :, got_rows]),
+            (r2_hbm.at[part, :], w2_s.at[slot, :, got_rows]),
         ]
         return [pltpu.make_async_copy(src, dst, w_sem.at[slot, i]) for i, (src, dst) in enumerate(pairs)]
 
     def grads(f, slot, ins):
-        cols = pl.ds(pl.multiple_of(f * FF_STEP, FF_STEP), FF_STEP)
+        cols = pl.ds(pl.multiple_of(f_base + f * FF_STEP, FF_STEP), FF_STEP)
         hbm = (i1, i3, i2) if ins else (o1, o3, o2)
         pairs = [
             (hbm[0].at[local, :, cols], d1_s.at[slot]),
@@ -477,6 +487,23 @@
 
         lax.fori_loop(0, n_tiles, load, 0)
 
+        def partial_sums(b, out):
+            rows = pl.ds(pl.multiple_of(b * CHUNK, CHUNK), CHUNK)
+            hbm_rows = pl.ds(pl.multiple_of((p * (PASS_TILES // CHUNK_TILES) + b) * CHUNK, CHUNK), CHUNK)
+            pairs = [(y_acc.at[rows, :], y_part.at[hbm_rows, :]), (du_acc.at[rows, :], du_part.at[hbm_rows, :])]
+            return [pltpu.make_async_copy(*(pair if out else pair[::-1]), part_sem) for pair in pairs]
+
+        def each_block(out, action):
+            def go(b, carry):
+                for cp in partial_sums(b, out):
+                    getattr(cp, action)()
+                return carry
+
+            lax.fori_loop(0, n_blk, go, 0)
+
+        if back and not first:
+            each_block(False, 'start')
+
         def fill(k, carry):
             u_s[rows_at(k), :] = jnp.zeros((TILE, width), BF16)
             dy_s[rows_at(k), :] = jnp.zeros((TILE, width), BF16)
@@ -497,6 +524,8 @@
             return carry
 
         lax.fori_loop(0, n_blk * CHUNK_TILES, flip, 0)
+        if back and not first:
+            each_block(False, 'wait')
         add = jnp.logical_or(p > 0, add_first > 0)
 
         def step(f, carry):
@@ -543,13 +572,17 @@
                     y = mm(g, w2)
                     du = mm(d_a, w1, NT) + mm(d_b, w3, NT)
 
-                    @pl.when(f == 0)
-                    def _():
-                        y_acc[rows, :] = y
-                        du_acc[rows, :] = du
-
-                    @pl.when(f > 0)
-                    def _():
+                    if first:
+                        @pl.when(f == 0)
+                        def _():
+                            y_acc[rows, :] = y
+                            du_acc[rows, :] = du
+
+                        @pl.when(f > 0)
+                        def _():
+                            y_acc[rows, :] += y
+                            du_acc[rows, :] += du
+                    else:
                         y_acc[rows, :] += y
                         du_acc[rows, :] += du
 
@@ -565,7 +598,10 @@
             return carry
 
         lax.fori_loop(0, n_ff, step, 0)
-        if back:
+        if back and not last:
+            each_block(True, 'start')
+            each_block(True, 'wait')
+        if back and last:
             def put(k, carry):
                 t = lst[0, p * PASS_TILES + k]
                 stage[0, rows_at(k), :] = y_acc[rows_at(k), :].astype(BF16)
@@ -589,7 +625,7 @@
 
     n_pass = jnp.maximum((total + (PASS_TILES - 1)) // PASS_TILES, 1)
     lax.fori_loop(0, n_pass, one_pass, 0)
-    if back:
+    if back and last:
         def cleared(t, carry):
             pltpu.make_async_copy(zero, tile_of(y_hbm, 0), row_sem).wait()
             pltpu.make_async_copy(zero, tile_of(du_hbm, 0), row_sem).wait()
@@ -598,10 +634,11 @@
         lax.fori_loop(0, n_src * CHUNK_TILES - total, cleared, 0)
 
 
-def experts(back, counts, prm, u_all, dy_all, own, got, dws):
+def experts(back, part, n_parts, counts, prm, u_all, dy_all, own, got, dws, sums=()):
     n_src, _, width = u_all.shape
+    first, last = part == 0, part == n_parts - 1
     hw = width // 2
-    ff = own[0].shape[2]
+    ff = got[1].shape[0]
     rows = PASS_TILES * TILE
     scratch = [
         pltpu.VMEM((rows, width), BF16),
@@ -620,28 +657,30 @@
         pltpu.SemaphoreType.DMA((2, 6)),
         pltpu.SemaphoreType.DMA((2, 3)),
     ]
-    outs = [jax.ShapeDtypeStruct(d.shape, d.dtype) for d in dws]
+    outs = [jax.ShapeDtypeStruct(d.shape, d.dtype) for d in (*dws, *sums)]
+    n_alias = len(outs)
+    if back and last:
+        outs += [jax.ShapeDtypeStruct(u_all.shape, BF16)] * 2
     if back:
-        outs += [jax.ShapeDtypeStruct(u_all.shape, BF16)] * 2
         scratch += [
             pltpu.VMEM((rows, width), F32),
             pltpu.VMEM((rows, width), F32),
             pltpu.VMEM((2, rows, width), BF16),
             pltpu.VMEM((TILE, width), BF16),
             pltpu.SemaphoreType.DMA,
+            pltpu.SemaphoreType.DMA,
         ]
     units = 7.5 if back else 4.5
     return pl.pallas_call(
-        functools.partial(experts_kernel, back, n_src),
+        functools.partial(experts_kernel, back, first, last, part * ff, n_src),
         out_shape=tuple(outs),
-        in_specs=[SMEM, SMEM] + [ANY] * 11,
+        in_specs=[SMEM, SMEM] + [ANY] * (7 + n_alias),
         out_specs=tuple([ANY] * len(outs)),
         scratch_shapes=scratch,
-        input_output_aliases={10: 0, 11: 1, 12: 2},
+        input_output_aliases={9 + i: i for i in range(n_alias)},
         compiler_params=params(),
-        cost_estimate=pl.CostEstimate(flops=int(units * 2 * 2 * CHUNK * width * ff), bytes_accessed=30 * 2**20, transcendentals=0),
-        name='experts_back' if back else 'experts_grad',
-    )(counts, prm, u_all, dy_all, *own, *got, *dws)
+        cost_estimate=pl.CostEstimate(flops=int(units * 2 * 2 * CHUNK * width * ff), bytes_accessed=10 * 2**20, transcendentals=0),
+    )(counts, prm, u_all, dy_all, *own, *got, *dws, *sums)
 
 
 def unset_kernel(*refs):
@@ -670,10 +709,26 @@
 
         def other(local):
             got = []
-            for w in own:
-                piece = lax.dynamic_index_in_dim(w, local, 0, keepdims=False)
-                got.append(lax.ppermute(piece, 'fsdp', swap))
+            gate, up, down = [lax.dynamic_index_in_dim(w, local, 0, keepdims=False) for w in own]
+            size = down.shape[0] // N_PARTS
+            for r in range(N_PARTS):
+                cols = slice(r * size, (r + 1) * size)
+                both = lax.ppermute(jnp.concatenate([gate[:, cols], up[:, cols]], axis=0), 'fsdp', swap)
+                got.append((both, lax.ppermute(down[cols], 'fsdp', swap)))
             return got
+
+        def back(chunk, add, u_c, dy_c, dws):
+            sums = unset(*[((n_dev * CHUNK, d_model), F32)] * 2)
+            for r in range(N_PARTS):
+                *state, = experts(True, r, N_PARTS, counts, prm(half, chunk, add), u_c, dy_c, own, got_mine[r], dws, sums)
+                dws, sums = state[:3], state[3:5]
+            return dws, state[5], state[6]
+
+        def grad_part(r, chunk, add, u_c, dy_c, dws):
+            return experts(False, r, N_PARTS, counts, prm(1 - half, chunk, add), u_c, dy_c, own, got_rest[r], dws)
+
+        def prm(local, chunk, add):
+            return jnp.stack([2 * col + local, local, half, chunk, add]).astype(jnp.int32)
 
         n_col = mesh.shape['ep']
         hw = w_qkv.shape[0]
@@ -692,20 +747,18 @@
         dy_all = lax.all_gather(pack(zero, counts, pos, gate, dout_tok, True), GROUP)
         got_rest = other(half)
 
-        h_tok, u_tok, qkv, ctx, lse, u_pack = attn_fwd(pos, w_all, x_tok, n_seq)
+        h_tok, u_tok, qkv, ctx, *probs, u_pack = attn_fwd(pos, w_all, x_tok, n_seq)
         u_all = lax.all_gather(u_pack, GROUP)
 
         tiles = (counts[:, :n_exp] + (TILE - 1)) // TILE
         n_chunks = jnp.max((jnp.sum(tiles, axis=1) + (CHUNK_TILES - 1)) // CHUNK_TILES)
         max_more = (n_tok + n_exp * (TILE - 1)) // CHUNK
 
-        def prm(local, chunk, add):
-            return jnp.stack([2 * col + local, local, half, chunk, add]).astype(jnp.int32)
-
         dws = unset(*[(w.shape, F32) for w in own])
         more_y, more_du = unset(*[((max_more, CHUNK, d_model), BF16)] * 2)
-        *dws, y_all, du_all = experts(True, counts, prm(half, zero, zero), u_all, dy_all, own, got_mine, dws)
+        dws, y_all, du_all = back(zero, zero, u_all, dy_all, dws)
         first_du = lax.psum_scatter(du_all, GROUP, scatter_dimension=0)
+
         first_y = lax.psum_scatter(y_all, GROUP, scatter_dimension=0)
 
         def fetch(c):
@@ -714,7 +767,7 @@
         def more_back(state):
             c, d1, d3, d2, ys, dus = state
             u_c, dy_c = fetch(c)
-            d1, d3, d2, y_c, du_c = experts(True, counts, prm(half, c, jnp.int32(1)), u_c, dy_c, own, got_mine, (d1, d3, d2))
+            (d1, d3, d2), y_c, du_c = back(c, jnp.int32(1), u_c, dy_c, (d1, d3, d2))
             y_c = lax.psum_scatter(y_c, GROUP, scatter_dimension=0)
             du_c = lax.psum_scatter(du_c, GROUP, scatter_dimension=0)
             ys = lax.dynamic_update_index_in_dim(ys, y_c, c - 1, 0)
@@ -724,14 +777,17 @@
         def more_grad(state):
             c, d1, d3, d2 = state
             u_c, dy_c = fetch(c)
-            d1, d3, d2 = experts(False, counts, prm(1 - half, c, jnp.int32(1)), u_c, dy_c, own, got_rest, (d1, d3, d2))
-            return c + 1, d1, d3, d2
+            dws = (d1, d3, d2)
+            for r in range(N_PARTS):
+                dws = grad_part(r, c, jnp.int32(1), u_c, dy_c, dws)
+            return (c + 1, *dws)
 
         _, *dws, more_y, more_du = lax.while_loop(lambda s: s[0] < n_chunks, more_back, (jnp.int32(1), *dws, more_y, more_du))
         layer_out = unpack(n_chunks, pos, gate, h_tok, first_y, more_y).reshape(n_seq, seq_len, d_model)
-        d_tokens = attn_bwd(n_chunks, pos, first_du, more_du, w_all, x_tok, h_tok, dout_tok, qkv, ctx, lse, n_seq).reshape(n_seq, seq_len, d_model)
-
-        dws = experts(False, counts, prm(1 - half, zero, zero), u_all, dy_all, own, got_rest, dws)
+        d_tokens = attn_bwd(n_chunks, pos, first_du, more_du, w_all, x_tok, h_tok, dout_tok, qkv, ctx, probs, n_seq).reshape(n_seq, seq_len, d_model)
+
+        for r in range(N_PARTS):
+            dws = grad_part(r, zero, zero, u_all, dy_all, dws)
         _, *dws = lax.while_loop(lambda s: s[0] < n_chunks, more_grad, (jnp.int32(1), *dws))
         return layer_out, d_tokens, *dws
 

time: 821 us -> 743 us (0.905)
  waiting for transfers between devices: 402 us -> 311 us
  starting transfers between devices: 40.4 us -> 23 us
  other arithmetic: 2.93 us -> 13.5 us
  Pallas kernels: 329 us -> 339 us
  local copies, waits for them, and re-layouts: 16.4 us -> 25.7 us
    ppermute x6 -> x12, waiting for transfers between devices: 390 us -> 298 us  [the longest x6 199 us: other(): got.append((both, lax.ppermute(down[cols], 'fsdp', swap)))]
    pallas_call x2 -> x6, Pallas kernels: 87.8 us -> 111 us  [experts(): pl.pallas_call(functools.partial(experts_kernel, back, first, last, part...]
    ppermute x6 -> x12, starting transfers between devices: 39.7 us -> 22.6 us  [the longest x6 17.7 us: other(): lax.ppermute(jnp.concatenate([gate[:, cols], up[:, cols]], axis=0), 'fsdp...]
    pallas_call x1, Pallas kernels: 113 us -> 98.4 us  [attn_bwd(): pl.pallas_call(attn_bwd_kernel, grid=(n_seq,), out_shape=jax.ShapeDtypeSt...]
    slice x0 -> x5, local copies, waits for them, and re-layouts: none -> 12.2 us  [the longest x1 4.6 us: other(): got.append((both, lax.ppermute(down[cols], 'fsdp', swap)))]
    concatenate x0 -> x6, other arithmetic: none -> 10.7 us  [other(): jnp.concatenate([gate[:, cols], up[:, cols]], axis=0)]
  transfers between devices with their start and end apart: 11 -> 17, of which waited for: 7 -> 8; matrix products, arithmetic and copies ran while one was open for 2% -> 5% of each run, Pallas kernels for 21% -> 30%
where the time goes in v1:
time: 743 us; the launch traced here: 740 us
  Pallas kernels  339 us (46%)
  waiting for transfers between devices  311 us (42%)
  local copies, waits for them, and re-layouts  25.7 us (3%)
  starting transfers between devices  23 us (3%)
  between operations  14.2 us (2%)
  other arithmetic  13.5 us (2%)
  blocking collectives  12.1 us (2%)
    ppermute x6, waiting for transfers between devices, other(): got.append((both, lax.ppermute(down[cols], 'fsdp', swap)))  199 us
    pallas_call x6, Pallas kernels, experts(): pl.pallas_call(functools.partial(experts_kernel, back, first, last, part...  111 us
    pallas_call x1, Pallas kernels, attn_fwd(): pl.pallas_call(attn_fwd_kernel, grid=(n_seq,), out_shape=(jax.ShapeDtypeS...  106 us
    ppermute x6, waiting for transfers between devices, other(): lax.ppermute(jnp.concatenate([gate[:, cols], up[:, cols]], axis=0), 'fsdp...  99 us
    pallas_call x1, Pallas kernels, attn_bwd(): pl.pallas_call(attn_bwd_kernel, grid=(n_seq,), out_shape=jax.ShapeDtypeSt...  98.4 us
    ppermute x6, starting transfers between devices, other(): lax.ppermute(jnp.concatenate([gate[:, cols], up[:, cols]], axis=0), 'fsdp...  17.7 us
  transfers between devices with their start and end apart: 17, of which 8 were waited for; matrix products, arithmetic and copies ran while one was open for 5% of the time, Pallas kernels for 30%

profile of v1, /device:TPU:0, one launch (start us, length us, event | category | flops | bytes accessed | tf_op | source)
XLA Modules:
  0.0 739.6 jit_solution(4760950118895504769)
XLA Ops:
  7.2 0.0 all-gather.28.cloned.1.call-start
  7.2 1.4 copy-done
  8.6 0.2 constant_dynamic-slice_fusion.2
  8.9 0.2 copy.66
  9.1 0.9 constant_dynamic-slice_fusion
  10.1 0.9 pad_maximum_fusion.6
  11.0 0.0 all-gather.32.cloned.1.call-start
  11.0 0.7 reshape.83.gate_ref
  11.7 2.4 route.1
  14.1 0.6 reshape.78.pos_ref
  14.7 12.1 %all-gather.7 = s32[8,1,128]{2,1,0:T(1,128)S(1)} all-gather(s32[1,1,128]{2,1,0:T(1,128)} %bitcast.124), channel_id=1, replica_groups=mesh['data'=1,'fsdp'=2,'ep'=4] {'fsdp','ep'}, dimensions={0}, use_global_device_ids=true | all-gather | bytes 4608 | tf_op jit(solution)/shard_map/all_gather | solution.py:742
  26.8 8.1 %pack.21 = bf16[640,768]{1,0:T(8,128)(2,1)} custom-call(s32[1]{0:T(128)} %constant.126.clone.1.c_ref, s32[8,128]{1,0:T(8,128)S(1)} %bitcast.114, s32[4,1024]{1,0:T(4,128)} %reshape.78.pos_ref, f32[4,1024]{1,0:T(4,128)S(1)} %reshape.83.gate_ref, bf16[4096,768]{1,0:T(8,128)(2,1)} %bitcast.127), custom_call_target="tpu_custom_call" | custom-call | flops 4026531840 | bytes 6291456 | tf_op jit(solution)/shard_map/pack/pallas_call | solution.py:100
  35.0 0.2 all-gather.30.cloned.1.call-start
  35.2 0.6 reshape.74.pos_ref
  35.8 11.4 %all-gather.28.cloned.1.call-done = bf16[768,3072]{1,0:T(8,128)(2,1)} async-done(((bf16[96,3072]{1,0:T(8,128)(2,1)}), bf16[768,3072]{1,0:T(8,128)(2,1)}) %all-gather.28.cloned.1.call-update) | async-done | bytes 4718608 | tf_op jit(solution)/shard_map/all_gather | solution.py:739
  47.2 106.3 %attn_fwd.1 = (bf16[4096,768]{1,0:T(8,128)(2,1)}, bf16[4096,768]{1,0:T(8,128)(2,1)}, bf16[4096,2304]{1,0:T(8,128)(2,1)}, bf16[4096,768]{1,0:T(8,128)(2,1)}, bf16...) custom-call(s32[8,512]{1,0:T(8,128)} %reshape.74.pos_ref, ...), custom_call_target="tpu_custom_call" | custom-call | flops 30000001024 | bytes 52428800 | tf_op jit(solution)/shard_map/attn_fwd/pallas_call | solution.py:270
  153.5 7.2 dynamic-slice_bitcast_fusion
  160.8 1.1 fusion.7
  161.9 1.1 fusion.6
  163.0 1.3 pad_maximum_fusion.2
  164.2 1.2 collective-permute-start.4
  165.5 4.6 dynamic-slice_bitcast_fusion.4
  170.1 0.8 collective-permute-start.5
  170.9 1.2 collective-permute-start.3
  172.1 0.8 collective-permute-start.1
  172.9 1.2 pad_maximum_fusion.1
  174.1 1.2 collective-permute-start.2
  175.4 0.1 fusion.1
  175.5 0.6 fusion.3
  176.1 0.6 pad_add_fusion
  176.7 2.7 pad_maximum_fusion
  179.4 64.8 %collective-permute-done.5.r2_hbm = bf16[1024,384]{1,0:T(8,128)(2,1)} collective-permute-done((bf16[1024,384]{1,0:T(8,128)(2,1)}, bf16[1024,384]{1,0:T(8,128)(2,1)}, u32[]{:S(2)}, u32[]{:S(2)}) %collective-permute-start.5) | collective-permute-done | bytes 786464 | tf_op jit(solution)/shard_map/ppermute | solution.py:717
  244.3 0.3 collective-permute-start
  244.6 17.8 %shard_map.137 = (f32[2,384,3072]{2,1,0:T(8,128)}, f32[2,384,3072]{2,1,0:T(8,128)}, f32[2,3072,384]{2,1,0:T(8,128)}, f32[5120,768]{1,0:T(8,128)}, f32[5120,768]{1,0:T(8,128)}) custom-call(s32[8,128]{1,0:T(8,128)S(1)} %bitcast.116, s32[5]{0:T(128)} %get-tuple-element.924.prm_ref, ...), custom_call_target="tpu_custom_call", output_to_operand_aliasing={{0}: (9, {}), {1}: (10, {}), {2}: (11, {}), {3}: (12, {}), ... | custom-call | flops 15099494400 | bytes 10485760 | tf_op jit(solution)/shard_map/pallas_call | solution.py:674
  262.4 49.1 %collective-permute-done.2.r13_hbm = bf16[768,1024]{1,0:T(8,128)(2,1)S(1)} collective-permute-done((bf16[768,1024]{1,0:T(8,128)(2,1)}, bf16[768,1024]{1,0:T(8,128)(2,1)S(1)}, u32[]{:S(2)}, u32[]{:S(2)}) %collective-permute-start.2) | collective-permute-done | bytes 1572896 | tf_op jit(solution)/shard_map/ppermute | solution.py:716
  311.6 16.6 %shard_map.138 = (f32[2,384,3072]{2,1,0:T(8,128)}, f32[2,384,3072]{2,1,0:T(8,128)}, f32[2,3072,384]{2,1,0:T(8,128)}, f32[5120,768]{1,0:T(8,128)}, f32[5120,768]{1,0:T(8,128)}) custom-call(s32[8,128]{1,0:T(8,128)S(1)} %bitcast.117, s32[5]{0:T(128)} %get-tuple-element.924.prm_ref, ...), custom_call_target="tpu_custom_call", output_to_operand_aliasing={{0}: (9, {}), {1}: (10, {}), {2}: (11, {}), {3}: (12, {}), ... | custom-call | flops 15099494400 | bytes 10485760 | tf_op jit(solution)/shard_map/pallas_call | solution.py:674
  328.2 17.0 %collective-permute-done.r13_hbm = bf16[768,1024]{1,0:T(8,128)(2,1)} collective-permute-done((bf16[768,1024]{1,0:T(8,128)(2,1)}, bf16[768,1024]{1,0:T(8,128)(2,1)}, u32[]{:S(2)}, u32[]{:S(2)}) %collective-permute-start) | collective-permute-done | bytes 1572896 | tf_op jit(solution)/shard_map/ppermute | solution.py:716
  345.2 20.8 %shard_map.139 = (f32[2,384,3072]{2,1,0:T(8,128)}, f32[2,384,3072]{2,1,0:T(8,128)}, f32[2,3072,384]{2,1,0:T(8,128)}, f32[5120,768]{1,0:T(8,128)}, f32[5120,768]{...) custom-call(s32[8,128]{1,0:T(8,128)S(1)} %bitcast.118, ...), custom_call_target="tpu_custom_call", output_to_operand_aliasing={{0}: (9, {}), {1}: (10, {}), {2}: (11, {}), {3}: (12, {}), ... | custom-call | flops 15099494400 | bytes 10485760 | tf_op jit(solution)/shard_map/pallas_call | solution.py:674
  366.0 1.0 while.40
  366.9 0.0 reduce-scatter.5.cloned.1.call-start
  367.0 0.5 reduce-scatter.5.cloned.1.call-update
  367.5 0.0 reduce-scatter.7.cloned.1.call-start
  367.6 0.5 reduce-scatter.7.cloned.1.call-update
  368.1 2.7 fusion.5
  370.8 2.7 fusion.4
  373.5 1.3 pad_maximum_fusion.5
  374.9 10.4 %collective-permute-start.10 = (bf16[768,1024]{1,0:T(8,128)(2,1)}, bf16[768,1024]{1,0:T(8,128)(2,1)S(1)}, u32[]{:S(2)}, u32[]{:S(2)}) collective-permute-start(bf16[768,1024]{1,0:T(8,128)(2,1)} %pad_maximum_fusion.5), channel_id=1, source_target_pairs={{0,4},{4,0},{1,5},{5,1},{2,6},{6,2},{3,7},{7,3}} | collective-permute-start | bytes 4718600 | tf_op jit(solution)/shard_map/ppermute | solution.py:716
  385.3 1.3 pad_maximum_fusion.4
  386.6 2.0 collective-permute-start.8
  388.6 2.0 collective-permute-start.7
  390.6 2.9 pad_maximum_fusion.3
  393.5 0.6 convert_bitcast_fusion.gate_ref
  394.1 74.4 %collective-permute-done.11.r2_hbm = bf16[1024,384]{1,0:T(8,128)(2,1)} collective-permute-done((bf16[1024,384]{1,0:T(8,128)(2,1)}, bf16[1024,384]{1,0:T(8,128)(2,1)}, u32[]{:S(2)}, u32[]{:S(2)}) %collective-permute-start.11) | collective-permute-done | bytes 786464 | tf_op jit(solution)/shard_map/ppermute | solution.py:717
  468.6 2.5 collective-permute-start.6
  471.1 18.4 %shard_map.140 = (f32[2,384,3072]{2,1,0:T(8,128)}, f32[2,384,3072]{2,1,0:T(8,128)}, f32[2,3072,384]{2,1,0:T(8,128)}) custom-call(s32[8,128]{1,0:T(8,128)S(1)} %get-tuple-element.1677, s32[5]{0:T(128)} %get-tuple-element.923.prm_ref, bf16[8,640,768]{2,1,0:T(8,128)(2,1)} %bitcast.110, ...), custom_call_target="tpu_custom_call", output_to_operand_aliasing={{0}: (9, {}), {1}: (10, {}), {2}: (11, {})} | custom-call | flops 9059696640 | bytes 10485760 | tf_op jit(solution)/shard_map/pallas_call | solution.py:674
  489.5 51.4 %collective-permute-done.9.r2_hbm = bf16[1024,384]{1,0:T(8,128)(2,1)} collective-permute-done((bf16[1024,384]{1,0:T(8,128)(2,1)}, bf16[1024,384]{1,0:T(8,128)(2,1)}, u32[]{:S(2)}, u32[]{:S(2)}) %collective-permute-start.9) | collective-permute-done | bytes 786464 | tf_op jit(solution)/shard_map/ppermute | solution.py:717
  540.9 19.1 %shard_map.141 = (f32[2,384,3072]{2,1,0:T(8,128)}, f32[2,384,3072]{2,1,0:T(8,128)}, f32[2,3072,384]{2,1,0:T(8,128)}) custom-call(s32[8,128]{1,0:T(8,128)S(1)} %get-tuple-element.1677, s32[5]{0:T(128)} %get-tuple-element.923.prm_ref, bf16[8,640,768]{2,1,0:T(8,128)(2,1)} %bitcast.111, ...), custom_call_target="tpu_custom_call", output_to_operand_aliasing={{0}: (9, {}), {1}: (10, {}), {2}: (11, {})} | custom-call | flops 9059696640 | bytes 10485760 | tf_op jit(solution)/shard_map/pallas_call | solution.py:674
  560.0 8.3 %collective-permute-done.7.r2_hbm = bf16[1024,384]{1,0:T(8,128)(2,1)} collective-permute-done((bf16[1024,384]{1,0:T(8,128)(2,1)}, bf16[1024,384]{1,0:T(8,128)(2,1)}, u32[]{:S(2)}, u32[]{:S(2)}) %collective-permute-start.7) | collective-permute-done | bytes 786464 | tf_op jit(solution)/shard_map/ppermute | solution.py:717
  568.3 32.9 %collective-permute-done.6.r13_hbm = bf16[768,1024]{1,0:T(8,128)(2,1)} collective-permute-done((bf16[768,1024]{1,0:T(8,128)(2,1)}, bf16[768,1024]{1,0:T(8,128)(2,1)}, u32[]{:S(2)}, u32[]{:S(2)}) %collective-permute-start.6) | collective-permute-done | bytes 1572896 | tf_op jit(solution)/shard_map/ppermute | solution.py:716
  601.2 18.8 %shard_map.142 = (f32[2,384,3072]{2,1,0:T(8,128)}, f32[2,384,3072]{2,1,0:T(8,128)}, f32[2,3072,384]{2,1,0:T(8,128)}) custom-call(s32[8,128]{1,0:T(8,128)S(1)} %get-tuple-element.1677, s32[5]{0:T(128)} %get-tuple-element.923.prm_ref, bf16[8,640,768]{2,1,0:T(8,128)(2,1)} %bitcast.112, ...), custom_call_target="tpu_custom_call", output_to_operand_aliasing={{0}: (9, {}), {1}: (10, {}), {2}: (11, {})} | custom-call | flops 9059696640 | bytes 10485760 | tf_op jit(solution)/shard_map/pallas_call | solution.py:674
  620.1 12.3 %unpack.1 = bf16[4096,768]{1,0:T(8,128)(2,1)} custom-call(s32[1]{0:T(128)} %bitcast.15.n_ref, s32[8,512]{1,0:T(8,128)} %reshape.74.pos_ref, f32[8,512]{1,0:T(8,128)} %convert_bitcast_fusion.gate_ref, bf16[4096,768]{1,0:T(8,128)(2,1)} %get-tuple-element.763.refs_0_.h_ref, bf16[640,768]{1,0:T(8,128)(2,1)} %bitcast.120, ...), custom_call_target="tpu_custom_call" | custom-call | flops 4026531840 | bytes 12582912 | tf_op jit(solution)/shard_map/unpack/pallas_call | solution.py:152
  632.4 98.4 %attn_bwd.1 = bf16[4096,768]{1,0:T(8,128)(2,1)} custom-call(s32[1]{0:T(128)} %bitcast.15.n_ref, s32[8,512]{1,0:T(8,128)} %reshape.74.pos_ref, bf16[640,768]{1,0:T(8,128)(2,1)} %bitcast.131, bf16[7,640,768]{2,1,0:T(8,128)(2,1)} %get-tuple-element.789.more_hbm, bf16[8,96,3072]{2,1,0:T(8,128)(2,1)} %bitcast.130, bf16[4096,768]{1,0:T(8,128)(2,1)} %bitcast.126, ...), custom_call_target="tpu_custom_call" | custom-call | flops 49999998976 | bytes 62914560 | tf_op jit(solution)/shard_map/attn_bwd/pallas_call | solution.py:367
  730.8 0.6 while.41
  731.4 1.5 copy-done.1
  (28 shorter events, 0.2 us)
Async XLA Ops:
  7.2 1.5 copy-start
  7.2 40.0 %all-gather.28.cloned.1.call-start = ((), (), s32[]{:S(2)}) async-start(), calls=%async_computation.6 | async-start | bytes 5308416 | tf_op jit(solution)/shard_map/all_gather | solution.py:739
  11.0 233.6 %all-gather.32.cloned.1.call-start = ((), (), s32[]{:S(2)}) async-start(), calls=%async_computation.8 | async-start | bytes 8847360 | tf_op jit(solution)/shard_map/all_gather | solution.py:747
  14.1 162.6 %copy-start.2 = (s32[32,128]{1,0:T(8,128)}, s32[32,128]{1,0:T(8,128)S(1)}, u32[]{:S(2)}) copy-start(s32[32,128]{1,0:T(8,128)S(1)} %get-tuple-element.1568) | copy-start | bytes 49156
  35.0 209.6 %all-gather.30.cloned.1.call-start = ((), (), s32[]{:S(2)}) async-start(), calls=%async_computation.7 | async-start | bytes 8847360 | tf_op jit(solution)/shard_map/all_gather | solution.py:751
  164.2 80.3 %collective-permute-start.4 = (bf16[768,1024]{1,0:T(8,128)(2,1)}, bf16[768,1024]{1,0:T(8,128)(2,1)S(1)}, u32[]{:S(2)}, u32[]{:S(2)}) collective-permute-start(bf16[768,1024]{1,0:T(8,128)(2,1)} %pad_maximum_fusion.2), channel_id=1, source_target_pairs={{0,4},{4,0},{1,5},{5,1},{2,6},{6,2},{3,7},{7,3}} | collective-permute-start | bytes 4718600 | tf_op jit(solution)/shard_map/ppermute | solution.py:716
  170.1 74.2 %collective-permute-start.5 = (bf16[1024,384]{1,0:T(8,128)(2,1)}, bf16[1024,384]{1,0:T(8,128)(2,1)}, u32[]{:S(2)}, u32[]{:S(2)}) collective-permute-start(bf16[1024,384]{1,0:T(8,128)(2,1)} %get-tuple-element.904), channel_id=1, source_target_pairs={{0,4},{4,0},{1,5},{5,1},{2,6},{6,2},{3,7},{7,3}} | collective-permute-start | bytes 2359304 | tf_op jit(solution)/shard_map/ppermute | solution.py:717
  170.9 91.5 %collective-permute-start.3 = (bf16[1024,384]{1,0:T(8,128)(2,1)}, bf16[1024,384]{1,0:T(8,128)(2,1)}, u32[]{:S(2)}, u32[]{:S(2)}) collective-permute-start(bf16[1024,384]{1,0:T(8,128)(2,1)} %get-tuple-element.902), channel_id=1, source_target_pairs={{0,4},{4,0},{1,5},{5,1},{2,6},{6,2},{3,7},{7,3}} | collective-permute-start | bytes 2359304 | tf_op jit(solution)/shard_map/ppermute | solution.py:717
  172.1 156.1 %collective-permute-start.1 = (bf16[1024,384]{1,0:T(8,128)(2,1)}, bf16[1024,384]{1,0:T(8,128)(2,1)}, u32[]{:S(2)}, u32[]{:S(2)}) collective-permute-start(bf16[1024,384]{1,0:T(8,128)(2,1)} %get-tuple-element.903), channel_id=1, source_target_pairs={{0,4},{4,0},{1,5},{5,1},{2,6},{6,2},{3,7},{7,3}} | collective-permute-start | bytes 2359304 | tf_op jit(solution)/shard_map/ppermute | solution.py:717
  174.1 137.4 %collective-permute-start.2 = (bf16[768,1024]{1,0:T(8,128)(2,1)}, bf16[768,1024]{1,0:T(8,128)(2,1)S(1)}, u32[]{:S(2)}, u32[]{:S(2)}) collective-permute-start(bf16[768,1024]{1,0:T(8,128)(2,1)} %pad_maximum_fusion.1), channel_id=1, source_target_pairs={{0,4},{4,0},{1,5},{5,1},{2,6},{6,2},{3,7},{7,3}} | collective-permute-start | bytes 4718600 | tf_op jit(solution)/shard_map/ppermute | solution.py:716
  244.3 100.9 %collective-permute-start = (bf16[768,1024]{1,0:T(8,128)(2,1)}, bf16[768,1024]{1,0:T(8,128)(2,1)}, u32[]{:S(2)}, u32[]{:S(2)}) collective-permute-start(bf16[768,1024]{1,0:T(8,128)(2,1)} %pad_maximum_fusion), channel_id=1, source_target_pairs={{0,4},{4,0},{1,5},{5,1},{2,6},{6,2},{3,7},{7,3}} | collective-permute-start | bytes 4718600 | tf_op jit(solution)/shard_map/ppermute | solution.py:716
  366.9 253.1 %reduce-scatter.5.cloned.1.call-start = ((), (), s32[]{:S(2)}) async-start(), calls=%async_computation.4 | async-start | bytes 8847360 | tf_op jit(solution)/shard_map/reduce_scatter | solution.py:762
  367.5 264.8 %reduce-scatter.7.cloned.1.call-start = ((), (), s32[]{:S(2)}) async-start(), calls=%async_computation.5 | async-start | bytes 8847360 | tf_op jit(solution)/shard_map/reduce_scatter | solution.py:760
  368.1 22.5 %copy-start.3 = (s32[32,128]{1,0:T(8,128)S(1)}, s32[32,128]{1,0:T(8,128)}, u32[]{:S(2)}) copy-start(s32[32,128]{1,0:T(8,128)} %get-tuple-element.1685) | copy-start | bytes 49156
  370.8 22.7 %copy-start.4 = (bf16[8,512,1]{1,0,2:T(8,128)(2,1)S(1)}, bf16[8,512,1]{1,0,2:T(8,128)(2,1)}, u32[]{:S(2)}) copy-start(bf16[8,512,1]{1,0,2:T(8,128)(2,1)} %param.22) | copy-start | bytes 24580
  374.9 96.2 %collective-permute-start.10 = (bf16[768,1024]{1,0:T(8,128)(2,1)}, bf16[768,1024]{1,0:T(8,128)(2,1)S(1)}, u32[]{:S(2)}, u32[]{:S(2)}) collective-permute-start(bf16[768,1024]{1,0:T(8,128)(2,1)} %pad_maximum_fusion.5), channel_id=1, source_target_pairs={{0,4},{4,0},{1,5},{5,1},{2,6},{6,2},{3,7},{7,3}} | collective-permute-start | bytes 4718600 | tf_op jit(solution)/shard_map/ppermute | solution.py:716
  385.3 83.3 %collective-permute-start.11 = (bf16[1024,384]{1,0:T(8,128)(2,1)}, bf16[1024,384]{1,0:T(8,128)(2,1)}, u32[]{:S(2)}, u32[]{:S(2)}) collective-permute-start(bf16[1024,384]{1,0:T(8,128)(2,1)} %get-tuple-element.899), channel_id=1, source_target_pairs={{0,4},{4,0},{1,5},{5,1},{2,6},{6,2},{3,7},{7,3}} | collective-permute-start | bytes 2359304 | tf_op jit(solution)/shard_map/ppermute | solution.py:717
  386.6 154.4 %collective-permute-start.8 = (bf16[768,1024]{1,0:T(8,128)(2,1)}, bf16[768,1024]{1,0:T(8,128)(2,1)S(1)}, u32[]{:S(2)}, u32[]{:S(2)}) collective-permute-start(bf16[768,1024]{1,0:T(8,128)(2,1)} %pad_maximum_fusion.4), channel_id=1, source_target_pairs={{0,4},{4,0},{1,5},{5,1},{2,6},{6,2},{3,7},{7,3}} | collective-permute-start | bytes 4718600 | tf_op jit(solution)/shard_map/ppermute | solution.py:716
  388.6 152.4 %collective-permute-start.9 = (bf16[1024,384]{1,0:T(8,128)(2,1)}, bf16[1024,384]{1,0:T(8,128)(2,1)}, u32[]{:S(2)}, u32[]{:S(2)}) collective-permute-start(bf16[1024,384]{1,0:T(8,128)(2,1)} %get-tuple-element.900), channel_id=1, source_target_pairs={{0,4},{4,0},{1,5},{5,1},{2,6},{6,2},{3,7},{7,3}} | collective-permute-start | bytes 2359304 | tf_op jit(solution)/shard_map/ppermute | solution.py:717
  388.6 179.7 %collective-permute-start.7 = (bf16[1024,384]{1,0:T(8,128)(2,1)}, bf16[1024,384]{1,0:T(8,128)(2,1)}, u32[]{:S(2)}, u32[]{:S(2)}) collective-permute-start(bf16[1024,384]{1,0:T(8,128)(2,1)} %get-tuple-element.901), channel_id=1, source_target_pairs={{0,4},{4,0},{1,5},{5,1},{2,6},{6,2},{3,7},{7,3}} | collective-permute-start | bytes 2359304 | tf_op jit(solution)/shard_map/ppermute | solution.py:717
  468.6 132.7 %collective-permute-start.6 = (bf16[768,1024]{1,0:T(8,128)(2,1)}, bf16[768,1024]{1,0:T(8,128)(2,1)}, u32[]{:S(2)}, u32[]{:S(2)}) collective-permute-start(bf16[768,1024]{1,0:T(8,128)(2,1)} %pad_maximum_fusion.3), channel_id=1, source_target_pairs={{0,4},{4,0},{1,5},{5,1},{2,6},{6,2},{3,7},{7,3}} | collective-permute-start | bytes 4718600 | tf_op jit(solution)/shard_map/ppermute | solution.py:716
  731.4 1.5 copy-start.1
Sparse Core Ops, SparseCore 0:
  11.1 36.0 all-gather.27
  49.0 46.4 all-gather.31
  153.6 72.6 all-gather.29
  370.8 101.8 reduce-scatter.4
  476.0 92.9 reduce-scatter.6

commit v2 on v1

--- a/solution.py
+++ b/solution.py
@@ -17,6 +17,7 @@
 FF_STEP = 512
 N_PARTS = 3
 GROUP = ('fsdp', 'ep')
+MESH = pl.DeviceIdType.MESH
 NN = (((1,), (0,)), ((), ()))
 NT = (((1,), (1,)), ((), ()))
 TN = (((0,), (0,)), ((), ()))
@@ -74,7 +75,7 @@
 PACK_STEP = 1024
 
 
-def pack_kernel(weighted, c_ref, cnt_ref, pos_ref, gate_ref, x_ref, out_ref, acc_ref):
+def pack_kernel(weighted, c_ref, pos_ref, gate_ref, x_ref, out_ref, acc_ref):
     k = pl.program_id(0)
     row = lax.broadcasted_iota(jnp.int32, (CHUNK, PACK_STEP), 0) + c_ref[0] * CHUNK
     hit = row == pos_ref[pl.ds(k, 1), :]
@@ -94,20 +95,20 @@
         out_ref[...] = acc_ref[...].astype(BF16)
 
 
-def pack(chunk, counts, pos, gate, x, weighted):
+def pack(chunk, pos, gate, x, weighted):
     n, width = x.shape
     steps = n // PACK_STEP
     return pl.pallas_call(
         functools.partial(pack_kernel, weighted),
         grid=(steps,),
         out_shape=jax.ShapeDtypeStruct((CHUNK, width), BF16),
-        in_specs=[SMEM, ANY, pl.BlockSpec((steps, PACK_STEP), lambda k: (0, 0)), pl.BlockSpec((steps, PACK_STEP), lambda k: (0, 0)), pl.BlockSpec((PACK_STEP, width), lambda k: (k, 0))],
+        in_specs=[SMEM, pl.BlockSpec((steps, PACK_STEP), lambda k: (0, 0)), pl.BlockSpec((steps, PACK_STEP), lambda k: (0, 0)), pl.BlockSpec((PACK_STEP, width), lambda k: (k, 0))],
         out_specs=pl.BlockSpec((CHUNK, width), lambda k: (0, 0)),
         scratch_shapes=[pltpu.VMEM((CHUNK, width), F32)],
         compiler_params=params(),
         cost_estimate=pl.CostEstimate(flops=2 * CHUNK * n * width, bytes_accessed=2 * n * width, transcendentals=0),
         name='pack',
-    )(chunk.reshape(1), counts, pos.reshape(steps, PACK_STEP), gate, x)
+    )(chunk.reshape(1), pos.reshape(steps, PACK_STEP), gate, x)
 
 
 UNPACK_STEP = 512
@@ -165,20 +166,132 @@
 QUERY_BLOCK = 256
 
 
-def load_attention_weights(w_hbm, wqkv, wo, sem):
-    n_dev, rows, _ = w_hbm.shape
-    wide, hw = wqkv.shape[1], wo.shape[2]
-    n_col = n_dev // 2
-    copies = []
-    for i in range(n_dev):
-        copies.append(pltpu.make_async_copy(w_hbm.at[i, :, pl.ds(0, wide)], wqkv.at[pl.ds(i * rows, rows), :], sem))
-        for j in range(2):
-            dst = wo.at[i // n_col, pl.ds((i % n_col * 2 + j) * rows, rows), :]
-            copies.append(pltpu.make_async_copy(w_hbm.at[i, :, pl.ds(wide + j * hw, hw)], dst, sem))
+def peers():
+    f, e = lax.axis_index('fsdp'), lax.axis_index('ep')
+    core = e + 1 - 2 * (e % 2)
+    return (f, e), (1 - f, e), (f, (e + 2) % 4), (f, core), (1 - f, (e + 2) % 4), (1 - f, core), (f, (core + 2) % 4), (1 - f, (core + 2) % 4)
+
+
+def rank(dev):
+    return dev[0] * 4 + dev[1]
+
+
+def meet_neighbours():
+    me, y, x, core, *_ = peers()
+    barrier = pltpu.get_barrier_semaphore()
+    for dev in (y, x, core):
+        pl.semaphore_signal(barrier, inc=1, device_id={'fsdp': dev[0], 'ep': dev[1]}, device_id_type=MESH)
+    pl.semaphore_wait(barrier, 3)
+
+
+def remote(src, dst, dev, sems, i):
+    return pltpu.make_async_remote_copy(src, dst, sems.at[0, i], sems.at[1, i], device_id={'fsdp': dev[0], 'ep': dev[1]}, device_id_type=MESH)
+
+
+class Gather:
+    def __init__(self, own, out, sems):
+        me, y, x, core, xy, *_ = peers()
+
+        def flow(i, src, owner, dev):
+            return remote(src, out.at[rank(owner)], dev, sems, i)
+
+        self.flows = [
+            flow(0, own, me, y),
+            flow(1, own, me, x),
+            flow(2, own, me, core),
+            flow(3, out.at[rank(y)], y, x),
+            flow(4, out.at[rank(y)], y, core),
+            flow(5, out.at[rank(x)], x, core),
+            flow(6, out.at[rank(xy)], xy, core),
+        ]
+        self.local = pltpu.make_async_copy(own, out.at[rank(me)], sems.at[0, 7])
+
+    def start(self):
+        for i in range(3):
+            self.flows[i].start()
+        self.local.start()
+
+    def forward_y(self):
+        self.flows[0].wait_recv()
+        self.flows[3].start()
+        self.flows[4].start()
+
+    def forward_x(self):
+        self.flows[1].wait_recv()
+        self.flows[5].start()
+
+    def forward_xy(self):
+        self.flows[3].wait_recv()
+        self.flows[6].start()
+
+    def finish(self):
+        for i in (2, 4, 5, 6):
+            self.flows[i].wait_recv()
+        for flow in self.flows:
+            flow.wait_send()
+        self.local.wait()
+
+    def run(self):
+        self.start()
+        self.forward_y()
+        self.forward_x()
+        self.forward_xy()
+        self.finish()
+
+
+def attention_weight_flows(wq_hbm, wo_hbm, wqkv, wo, sems):
+    me, y, x, core, xy, _, _, _ = peers()
+    hw = wq_hbm.shape[0]
+    quarter = hw // 4
+
+    def pieces(dev):
+        return wqkv.at[pl.ds(dev[0] * hw + dev[1] * quarter, quarter), :], wo.at[dev[0], pl.ds(dev[1] * 2 * quarter, 2 * quarter), :]
+
+    mine = wq_hbm.at[pl.ds(me[1] * quarter, quarter), :], wo_hbm.at[pl.ds(me[1] * 2 * quarter, 2 * quarter), :]
+    flows = []
+    for part in range(2):
+        flows.append([
+            remote(mine[part], pieces(me)[part], y, sems, part),
+            remote(pieces(y)[part], pieces(y)[part], x, sems, 2 + part),
+            remote(pieces(y)[part], pieces(y)[part], core, sems, 4 + part),
+            remote(pieces(xy)[part], pieces(xy)[part], core, sems, 6 + part),
+        ])
+    return flows
+
+
+def load_attention_weights(wqkv_hbm, wo_hbm, wqkv, wo, sems):
+    copies = [pltpu.make_async_copy(wqkv_hbm, wqkv, sems.at[0]), pltpu.make_async_copy(wo_hbm, wo, sems.at[1])]
     for cp in copies:
         cp.start()
     for cp in copies:
         cp.wait()
+
+
+class WeightPieces:
+    def __init__(self, own, send, part, outs, sems, n):
+        y = peers()[1]
+        gate, up, down = own
+        r13, r2 = outs
+        hw, size = gate.shape[1], r2.shape[0]
+        cols = pl.ds(part * size, size)
+        step, step2 = hw // n, size // n
+        self.pieces = []
+        for i in range(n):
+            rows = pl.ds(i * step, step)
+            self.pieces.append([
+                remote(gate.at[send, rows, cols], r13.at[rows, :], y, sems, 3 * i),
+                remote(up.at[send, rows, cols], r13.at[pl.ds(hw + i * step, step), :], y, sems, 3 * i + 1),
+                remote(down.at[send, pl.ds(part * size + i * step2, step2), :], r2.at[pl.ds(i * step2, step2), :], y, sems, 3 * i + 2),
+            ])
+
+    def start(self, i):
+        for cp in self.pieces[i]:
+            cp.start()
+
+    def finish(self):
+        for piece in self.pieces:
+            for cp in piece:
+                cp.wait()
 
 
 def inv_rms_of(wide_vals):
@@ -198,15 +311,68 @@
     return tail if k == n else jnp.concatenate([values[:, : k - n], tail], axis=1)
 
 
-def attn_fwd_kernel(pos_ref, w_hbm, x_ref, h_ref, u_ref, qkv_ref, ctx_ref, p0_ref, p1_ref, pack_ref, wqkv, wo, acc, sem):
+def attn_fwd_kernel(pos_ref, cnt_hbm, dy_hbm, wq_hbm, wo_hbm, gate_hbm, up_hbm, down_hbm, x_ref, *refs):
+    h_ref, u_ref, qkv_ref, ctx_ref, p0_ref, p1_ref, wqkv_out, wo_out, cnt_all, dy_all, u_all, a0, b0, a1, b1 = refs[:15]
+    wqkv, wo, acc, u_pack, sem_a, sem_c, sem_d, sem_u, sem_0, sem_1, sem_w = refs[15:]
     i = pl.program_id(0)
     width = x_ref.shape[1]
     hw = width // 2
     seq = x_ref.shape[0]
+    me = peers()[0]
+    own = gate_hbm, up_hbm, down_hbm
+    counts, dys, us = Gather(cnt_hbm, cnt_all, sem_c), Gather(dy_hbm, dy_all, sem_d), Gather(u_pack, u_all, sem_u)
+    part0 = WeightPieces(own, 1 - me[0], 0, (a0, b0), sem_0, 1)
+    part1 = WeightPieces(own, 1 - me[0], 1, (a1, b1), sem_1, 4)
+    flows = attention_weight_flows(wq_hbm, wo_hbm, wqkv, wo, sem_a)
+    local = [
+        pltpu.make_async_copy(wq_hbm, wqkv.at[pl.ds(me[0] * hw, hw), :], sem_w.at[0]),
+        pltpu.make_async_copy(wo_hbm, wo.at[me[0]], sem_w.at[1]),
+    ]
+    keep = [pltpu.make_async_copy(wqkv, wqkv_out, sem_w.at[2]), pltpu.make_async_copy(wo, wo_out, sem_w.at[3])]
 
     @pl.when(i == 0)
     def _():
-        load_attention_weights(w_hbm, wqkv, wo, sem)
+        meet_neighbours()
+        for cps in flows:
+            cps[0].start()
+        for cp in local:
+            cp.start()
+        counts.start()
+        for cps in flows:
+            cps[0].wait_recv()
+            cps[1].start()
+            cps[2].start()
+        dys.start()
+        part0.start(0)
+        for cps in flows:
+            cps[1].wait_recv()
+            cps[3].start()
+        for cps in flows:
+            cps[2].wait_recv()
+            cps[3].wait_recv()
+            for cp in cps:
+                cp.wait_send()
+        for cp in local:
+            cp.wait()
+        for cp in keep:
+            cp.start()
+
+    @pl.when(i == 2)
+    def _():
+        counts.forward_y()
+        counts.forward_x()
+        dys.forward_y()
+        dys.forward_x()
+
+    @pl.when(i == 4)
+    def _():
+        counts.forward_xy()
+        dys.forward_xy()
+
+    for n in range(4):
+        @pl.when(i == 3 + n)
+        def _(n=n):
+            part1.start(n)
 
     x = x_ref[...].astype(F32)
     normed = (x * inv_rms_of(x)).astype(BF16)
@@ -252,7 +418,14 @@
 
     @pl.when(i == pl.num_programs(0) - 1)
     def _():
-        pack_ref[...] = acc[...].astype(BF16)
+        u_pack[...] = acc[...].astype(BF16)
+        us.run()
+        counts.finish()
+        dys.finish()
+        part0.finish()
+        part1.finish()
+        for cp in keep:
+            cp.wait()
 
 
 def probs_shapes(n_seq, width):
@@ -263,11 +436,15 @@
     return [pl.BlockSpec((1, width // 64, QUERY_BLOCK, (j + 1) * QUERY_BLOCK), lambda i: (i, 0, 0, 0)) for j in range(2)]
 
 
-def attn_fwd(pos, w_all, x, n_seq):
+def attn_fwd(pos, cnt, dy, wq, wo, own, x, n_seq):
     n, width = x.shape
     seq = n // n_seq
+    hw = width // 2
+    size = own[0].shape[2] // N_PARTS
     rows = pl.BlockSpec((seq, width), lambda i: (i, 0))
-    return pl.pallas_call(
+    part = [jax.ShapeDtypeStruct((width, size), BF16), jax.ShapeDtypeStruct((size, hw), BF16)]
+    sems = lambda k: pltpu.SemaphoreType.DMA((2, k))
+    h, u, qkv, ctx, p0, p1, *rest = pl.pallas_call(
         attn_fwd_kernel,
         grid=(n_seq,),
         out_shape=(
@@ -276,15 +453,34 @@
             jax.ShapeDtypeStruct((n, 3 * width), BF16),
             jax.ShapeDtypeStruct((n, width), BF16),
             *probs_shapes(n_seq, width),
-            jax.ShapeDtypeStruct((CHUNK, width), BF16),
+            jax.ShapeDtypeStruct((width, 3 * width), BF16),
+            jax.ShapeDtypeStruct((2, width, hw), BF16),
+            jax.ShapeDtypeStruct((8, 1, 128), jnp.int32),
+            jax.ShapeDtypeStruct((8, CHUNK, width), BF16),
+            jax.ShapeDtypeStruct((8, CHUNK, width), BF16),
+            *part,
+            *part,
         ),
-        in_specs=[pl.BlockSpec((n_seq, seq), lambda i: (0, 0)), ANY, rows],
-        out_specs=(rows, rows, pl.BlockSpec((seq, 3 * width), lambda i: (i, 0)), rows, *probs_specs(width), pl.BlockSpec((CHUNK, width), lambda i: (0, 0))),
-        scratch_shapes=[pltpu.VMEM((width, 3 * width), BF16), pltpu.VMEM((2, width, width // 2), BF16), pltpu.VMEM((CHUNK, width), F32), pltpu.SemaphoreType.DMA],
-        compiler_params=params(),
+        in_specs=[pl.BlockSpec((n_seq, seq), lambda i: (0, 0))] + [ANY] * 7 + [rows],
+        out_specs=(rows, rows, pl.BlockSpec((seq, 3 * width), lambda i: (i, 0)), rows, *probs_specs(width)) + (ANY,) * 9,
+        scratch_shapes=[
+            pltpu.VMEM((width, 3 * width), BF16),
+            pltpu.VMEM((2, width, hw), BF16),
+            pltpu.VMEM((CHUNK, width), F32),
+            pltpu.VMEM((CHUNK, width), BF16),
+            sems(8),
+            sems(8),
+            sems(8),
+            sems(8),
+            sems(3),
+            sems(12),
+            pltpu.SemaphoreType.DMA((4,)),
+        ],
+        compiler_params=pltpu.CompilerParams(vmem_limit_bytes=60 * 1024 * 1024, collective_id=0, has_side_effects=True),
         cost_estimate=pl.CostEstimate(flops=30 * 10**9, bytes_accessed=50 * 2**20, transcendentals=0),
         name='attn_fwd',
-    )(pos.reshape(n_seq, seq), w_all, x)
+    )(pos.reshape(n_seq, seq), cnt, dy, wq, wo, *own, x)
+    return (h, u, qkv, ctx, (p0, p1)), rest
 
 
 def norm_back(grad, wide_vals):
@@ -292,14 +488,14 @@
     return inv * (grad - wide_vals * (inv * inv * jnp.mean(grad * wide_vals, axis=-1, keepdims=True)))
 
 
-def attn_bwd_kernel(n_ref, pos_ref, first_ref, more_hbm, w_hbm, x_ref, h_ref, dout_ref, qkv_ref, ctx_ref, p0_ref, p1_ref, dx_ref, wqkv, wo, dqkv, dctx, dh, buf, sem):
+def attn_bwd_kernel(n_ref, pos_ref, first_ref, more_hbm, wqkv_hbm, wo_hbm, x_ref, h_ref, dout_ref, qkv_ref, ctx_ref, p0_ref, p1_ref, dx_ref, wqkv, wo, dqkv, dctx, dh, buf, sem, w_sem):
     i = pl.program_id(0)
     seq, width = x_ref.shape
     hw = width // 2
 
     @pl.when(i == 0)
     def _():
-        load_attention_weights(w_hbm, wqkv, wo, sem)
+        load_attention_weights(wqkv_hbm, wo_hbm, wqkv, wo, w_sem)
 
     pos = pos_ref[pl.ds(i, 1), :]
     row = lax.broadcasted_iota(jnp.int32, (CHUNK, seq), 0)
@@ -360,7 +556,7 @@
     dx_ref[...] = (dh[...] + norm_back(dn, x_ref[...].astype(F32))).astype(BF16)
 
 
-def attn_bwd(n_chunks, pos, first, more, w_all, x, h, dout, qkv, ctx, probs, n_seq):
+def attn_bwd(n_chunks, pos, first, more, wqkv, wo, x, h, dout, qkv, ctx, probs, n_seq):
     n, width = x.shape
     seq = n // n_seq
     rows = pl.BlockSpec((seq, width), lambda i: (i, 0))
@@ -368,7 +564,7 @@
         attn_bwd_kernel,
         grid=(n_seq,),
         out_shape=jax.ShapeDtypeStruct((n, width), BF16),
-        in_specs=[SMEM, pl.BlockSpec((n_seq, seq), lambda i: (0, 0)), pl.BlockSpec((CHUNK, width), lambda i: (0, 0)), ANY, ANY, rows, rows, rows, pl.BlockSpec((seq, 3 * width), lambda i: (i, 0)), rows, *probs_specs(width)],
+        in_specs=[SMEM, pl.BlockSpec((n_seq, seq), lambda i: (0, 0)), pl.BlockSpec((CHUNK, width), lambda i: (0, 0)), ANY, ANY, ANY, rows, rows, rows, pl.BlockSpec((seq, 3 * width), lambda i: (i, 0)), rows, *probs_specs(width)],
         out_specs=rows,
         scratch_shapes=[
             pltpu.VMEM((width, 3 * width), BF16),
@@ -378,11 +574,12 @@
             pltpu.VMEM((seq, width), F32),
             pltpu.VMEM((CHUNK, width), BF16),
             pltpu.SemaphoreType.DMA,
+            pltpu.SemaphoreType.DMA((2,)),
         ],
         compiler_params=params(),
         cost_estimate=pl.CostEstimate(flops=50 * 10**9, bytes_accessed=60 * 2**20, transcendentals=0),
         name='attn_bwd',
-    )(n_chunks.reshape(1), pos.reshape(n_seq, seq), first, more, w_all, x, h, dout, qkv, ctx, *probs)
+    )(n_chunks.reshape(1), pos.reshape(n_seq, seq), first, more, wqkv, wo, x, h, dout, qkv, ctx, *probs)
 
 
 def experts_kernel(back, first, last, f_base, n_src, cnt_ref, prm_ref, u_hbm, dy_hbm, w1_hbm, w3_hbm, w2_hbm, r13_hbm, r2_hbm, i1, i3, i2, *refs):
@@ -707,15 +904,12 @@
         swap = [(0, 1), (1, 0)]
         own = (w_gate, w_up, w_down)
 
-        def other(local):
-            got = []
+        def other(local, r):
             gate, up, down = [lax.dynamic_index_in_dim(w, local, 0, keepdims=False) for w in own]
             size = down.shape[0] // N_PARTS
-            for r in range(N_PARTS):
-                cols = slice(r * size, (r + 1) * size)
-                both = lax.ppermute(jnp.concatenate([gate[:, cols], up[:, cols]], axis=0), 'fsdp', swap)
-                got.append((both, lax.ppermute(down[cols], 'fsdp', swap)))
-            return got
+            cols = slice(r * size, (r + 1) * size)
+            both = lax.ppermute(jnp.concatenate([gate[:, cols], up[:, cols]], axis=0), 'fsdp', swap)
+            return both, lax.ppermute(down[cols], 'fsdp', swap)
 
         def back(chunk, add, u_c, dy_c, dws):
             sums = unset(*[((n_dev * CHUNK, d_model), F32)] * 2)
@@ -730,25 +924,18 @@
         def prm(local, chunk, add):
             return jnp.stack([2 * col + local, local, half, chunk, add]).astype(jnp.int32)
 
-        n_col = mesh.shape['ep']
-        hw = w_qkv.shape[0]
-        eighth = hw // n_col
-        qkv_part = lax.dynamic_slice_in_dim(w_qkv.reshape(hw, 3 * d_model), col * eighth, eighth, 0)
-        out_part = lax.dynamic_slice_in_dim(w_out.reshape(d_model, hw), col * 2 * eighth, 2 * eighth, 0)
-        w_part = jnp.concatenate([qkv_part, out_part[:eighth], out_part[eighth:]], axis=1)
-        w_all = lax.all_gather(w_part, GROUP)
         x_tok = tokens.reshape(n_tok, d_model)
+        dout_tok = d_out.reshape(n_tok, d_model)
+        gate = gate_wts.reshape(n_tok // PACK_STEP, PACK_STEP).astype(F32)
+        zero = jnp.int32(0)
         pos, cnt = route(expert_idx, expert_slot, n_exp)
-        counts = lax.all_gather(cnt[0], GROUP)
-        got_mine = other(1 - half)
-        gate = gate_wts.reshape(n_tok // PACK_STEP, PACK_STEP).astype(F32)
-        dout_tok = d_out.reshape(n_tok, d_model)
-        zero = jnp.int32(0)
-        dy_all = lax.all_gather(pack(zero, counts, pos, gate, dout_tok, True), GROUP)
-        got_rest = other(half)
-
-        h_tok, u_tok, qkv, ctx, *probs, u_pack = attn_fwd(pos, w_all, x_tok, n_seq)
-        u_all = lax.all_gather(u_pack, GROUP)
+        dy_pack = pack(zero, pos, gate, dout_tok, True)
+        wq = w_qkv.reshape(d_model // 2, 3 * d_model)
+        (h_tok, u_tok, qkv, ctx, probs), gathered = attn_fwd(pos, cnt, dy_pack, wq, w_out.reshape(d_model, d_model // 2), own, x_tok, n_seq)
+        wqkv_full, wo_full, counts, dy_all, u_all, a0, b0, a1, b1 = gathered
+        counts = counts.reshape(n_exp, 128)
+        got_mine = [(a0, b0), (a1, b1), other(1 - half, 2)]
+        got_rest = [other(half, r) for r in range(N_PARTS)]
 
         tiles = (counts[:, :n_exp] + (TILE - 1)) // TILE
         n_chunks = jnp.max((jnp.sum(tiles, axis=1) + (CHUNK_TILES - 1)) // CHUNK_TILES)
@@ -762,7 +949,7 @@
         first_y = lax.psum_scatter(y_all, GROUP, scatter_dimension=0)
 
         def fetch(c):
-            return lax.all_gather(pack(c, counts, pos, gate, u_tok, False), GROUP), lax.all_gather(pack(c, counts, pos, gate, dout_tok, True), GROUP)
+            return lax.all_gather(pack(c, pos, gate, u_tok, False), GROUP), lax.all_gather(pack(c, pos, gate, dout_tok, True), GROUP)
 
         def more_back(state):
             c, d1, d3, d2, ys, dus = state
@@ -784,7 +971,7 @@
 
         _, *dws, more_y, more_du = lax.while_loop(lambda s: s[0] < n_chunks, more_back, (jnp.int32(1), *dws, more_y, more_du))
         layer_out = unpack(n_chunks, pos, gate, h_tok, first_y, more_y).reshape(n_seq, seq_len, d_model)
-        d_tokens = attn_bwd(n_chunks, pos, first_du, more_du, w_all, x_tok, h_tok, dout_tok, qkv, ctx, probs, n_seq).reshape(n_seq, seq_len, d_model)
+        d_tokens = attn_bwd(n_chunks, pos, first_du, more_du, wqkv_full, wo_full, x_tok, h_tok, dout_tok, qkv, ctx, probs, n_seq).reshape(n_seq, seq_len, d_model)
 
         for r in range(N_PARTS):
             dws = grad_part(r, zero, zero, u_all, dy_all, dws)

time: 743 us -> 711 us (0.957)
  waiting for transfers between devices: 311 us -> 169 us
  Pallas kernels: 339 us -> 449 us
  starting transfers between devices: 23 us -> 45.1 us
  blocking collectives: 12.1 us -> 0 us
  local copies, waits for them, and re-layouts: 25.7 us -> 17.2 us
    pallas_call x1, Pallas kernels: 106 us -> 216 us  [attn_fwd(): pl.pallas_call(attn_fwd_kernel, grid=(n_seq,), out_shape=(jax.ShapeDtypeS...]
    ppermute x6 -> x4, waiting for transfers between devices: 99 us -> 33.9 us  [other(): lax.ppermute(jnp.concatenate([gate[:, cols], up[:, cols]], axis=0), 'fsdp...]
    ppermute x6 -> x4, waiting for transfers between devices: 199 us -> 134 us  [other(): return (both, lax.ppermute(down[cols], 'fsdp', swap))]
    ppermute x6 -> x4, starting transfers between devices: 17.7 us -> 39.7 us  [other(): lax.ppermute(jnp.concatenate([gate[:, cols], up[:, cols]], axis=0), 'fsdp...]
    all_gather x1 -> x0, blocking collectives: 12.1 us -> none  [device_fn(): counts = lax.all_gather(cnt[0], GROUP)]
    all_gather x3 -> x0, waiting for transfers between devices: 11.4 us -> none  [the longest x1 11.4 us: device_fn(): w_all = lax.all_gather(w_part, GROUP)]
  transfers between devices with their start and end apart: 17 -> 10, of which waited for: 8 -> 4; matrix products, arithmetic and copies ran while one was open for 5% -> 3% of each run, Pallas kernels for 30% -> 47%
where the time goes in v2:
time: 711 us; the launch traced here: 707 us
  Pallas kernels  449 us (63%)
  waiting for transfers between devices  169 us (24%)
  starting transfers between devices  45.1 us (6%)
  local copies, waits for them, and re-layouts  17.2 us (2%)
  between operations  15.9 us (2%)
  other arithmetic  8.73 us (1%)
    pallas_call x1, Pallas kernels, attn_fwd(): pl.pallas_call(attn_fwd_kernel, grid=(n_seq,), out_shape=(jax.ShapeDtypeS...  216 us
    ppermute x4, waiting for transfers between devices, other(): return (both, lax.ppermute(down[cols], 'fsdp', swap))  134 us
    pallas_call x6, Pallas kernels, experts(): pl.pallas_call(functools.partial(experts_kernel, back, first, last, part...  111 us
    pallas_call x1, Pallas kernels, attn_bwd(): pl.pallas_call(attn_bwd_kernel, grid=(n_seq,), out_shape=jax.ShapeDtypeSt...  98.3 us
    ppermute x4, starting transfers between devices, other(): lax.ppermute(jnp.concatenate([gate[:, cols], up[:, cols]], axis=0), 'fsdp...  39.7 us
    ppermute x4, waiting for transfers between devices, other(): lax.ppermute(jnp.concatenate([gate[:, cols], up[:, cols]], axis=0), 'fsdp...  33.9 us
  transfers between devices with their start and end apart: 10, of which 4 were waited for; matrix products, arithmetic and copies ran while one was open for 3% of the time, Pallas kernels for 47%

profile of v2, /device:TPU:0, one launch (start us, length us, event | category | flops | bytes accessed | tf_op | source)
XLA Modules:
  0.0 706.6 jit_solution(1598524783000364423)
XLA Ops:
  8.0 0.0 copy-start
  8.0 3.8 dynamic-slice_bitcast_fusion.4
  11.8 0.0 copy-start.5
  11.8 0.0 copy-start.2
  11.8 3.3 collective-permute-start.1
  15.1 0.0 copy-done
  15.1 5.8 dynamic-slice_bitcast_fusion
  20.9 0.1 slice.69
  21.0 0.1 slice.68
  21.0 1.2 pad_maximum_fusion
  22.3 0.2 collective-permute-start
  22.5 2.4 route.1
  24.9 0.6 reshape.74.pos_ref
  25.5 0.6 reshape.75.pos_ref
  26.1 0.0 copy-done.5
  26.2 0.0 copy-done.2
  26.2 2.4 copy.64.wq_hbm
  28.5 8.0 %pack.21.dy_hbm = bf16[640,768]{1,0:T(8,128)(2,1)} custom-call(s32[1]{0:T(128)} %constant.118.clone.1.c_ref, s32[4,1024]{1,0:T(4,128)} %reshape.75.pos_ref, f32[4,1024]{1,0:T(4,128)S(1)} %reshape.84.gate_ref, bf16[4096,768]{1,0:T(8,128)(2,1)} %bitcast.104), custom_call_target="tpu_custom_call" | custom-call | flops 4026531840 | bytes 6291456 | tf_op jit(solution)/shard_map/pack/pallas_call | solution.py:101
  36.5 0.6 pad_add_fusion
  37.1 216.5 %attn_fwd.1 = (bf16[4096,768]{1,0:T(8,128)(2,1)}, bf16[4096,768]{1,0:T(8,128)(2,1)}, bf16[4096,2304]{1,0:T(8,128)(2,1)}, bf16[4096,768]{1,0:T(8,128)(2,1)}, bf16...) custom-call(s32[8,512]{1,0:T(8,128)} %reshape.74.pos_ref, ...), custom_call_target="tpu_custom_call" | custom-call | flops 30000001024 | bytes 52428800 | tf_op jit(solution)/shard_map/attn_fwd/pallas_call | solution.py:447
  253.6 18.2 %shard_map.137 = (f32[2,384,3072]{2,1,0:T(8,128)}, f32[2,384,3072]{2,1,0:T(8,128)}, f32[2,3072,384]{2,1,0:T(8,128)}, f32[5120,768]{1,0:T(8,128)}, f32[5120,768]{1,0:T(8,128)}) custom-call(s32[8,128]{1,0:T(8,128)S(1)} %bitcast.93, s32[5]{0:T(128)} %get-tuple-element.930.prm_ref, ...), custom_call_target="tpu_custom_call", output_to_operand_aliasing={{0}: (9, {}), {1}: (10, {}), {2}: (11, {}), {3}: (12, {}), ... | custom-call | flops 15099494400 | bytes 10485760 | tf_op jit(solution)/shard_map/pallas_call | solution.py:871
  271.8 0.1 fusion.1
  271.9 0.0 copy-done.3
  271.9 0.7 fusion.3
  272.6 16.6 %shard_map.138 = (f32[2,384,3072]{2,1,0:T(8,128)}, f32[2,384,3072]{2,1,0:T(8,128)}, f32[2,3072,384]{2,1,0:T(8,128)}, f32[5120,768]{1,0:T(8,128)}, f32[5120,768]{1,0:T(8,128)}) custom-call(s32[8,128]{1,0:T(8,128)S(1)} %bitcast.95, s32[5]{0:T(128)} %get-tuple-element.930.prm_ref, ...), custom_call_target="tpu_custom_call", output_to_operand_aliasing={{0}: (9, {}), {1}: (10, {}), {2}: (11, {}), {3}: (12, {}), ... | custom-call | flops 15099494400 | bytes 10485760 | tf_op jit(solution)/shard_map/pallas_call | solution.py:871
  289.2 0.0 collective-permute-done.1.r2_hbm
  289.2 0.0 collective-permute-done.r13_hbm
  289.2 20.8 %shard_map.139 = (f32[2,384,3072]{2,1,0:T(8,128)}, f32[2,384,3072]{2,1,0:T(8,128)}, f32[2,3072,384]{2,1,0:T(8,128)}, f32[5120,768]{1,0:T(8,128)}, f32[5120,768]{...) custom-call(s32[8,128]{1,0:T(8,128)S(1)} %bitcast.96, ...), custom_call_target="tpu_custom_call", output_to_operand_aliasing={{0}: (9, {}), {1}: (10, {}), {2}: (11, {}), {3}: (12, {}), ... | custom-call | flops 15099494400 | bytes 10485760 | tf_op jit(solution)/shard_map/pallas_call | solution.py:871
  310.0 1.0 while.40
  311.1 0.0 reduce-scatter.5.cloned.1.call-start
  311.1 0.5 reduce-scatter.5.cloned.1.call-update
  311.6 0.0 copy-start.1
  311.7 0.0 reduce-scatter.7.cloned.1.call-start
  311.7 0.5 reduce-scatter.7.cloned.1.call-update
  312.3 0.0 copy-start.4
  312.3 2.8 fusion.5
  315.1 0.0 copy-done.1
  315.1 1.1 fusion.4
  316.1 1.3 pad_maximum_fusion.3
  317.4 34.9 %collective-permute-start.6 = (bf16[768,1024]{1,0:T(8,128)(2,1)}, bf16[768,1024]{1,0:T(8,128)(2,1)S(1)}, u32[]{:S(2)}, u32[]{:S(2)}) collective-permute-start(bf16[768,1024]{1,0:T(8,128)(2,1)} %pad_maximum_fusion.3), channel_id=1, source_target_pairs={{0,4},{4,0},{1,5},{5,1},{2,6},{6,2},{3,7},{7,3}} | collective-permute-start | bytes 4718600 | tf_op jit(solution)/shard_map/ppermute | solution.py:911
  352.4 0.0 collective-permute-start.7
  352.4 1.3 pad_maximum_fusion.2
  353.7 2.0 collective-permute-start.4
  355.7 0.0 collective-permute-start.5
  355.7 2.0 collective-permute-start.3
  357.7 0.0 copy-done.4
  357.7 2.9 pad_maximum_fusion.1
  360.6 0.0 copy-done.6
  360.6 0.6 convert_bitcast_fusion.gate_ref
  361.3 72.9 %collective-permute-done.7.r2_hbm = bf16[1024,384]{1,0:T(8,128)(2,1)} collective-permute-done((bf16[1024,384]{1,0:T(8,128)(2,1)}, bf16[1024,384]{1,0:T(8,128)(2,1)}, u32[]{:S(2)}, u32[]{:S(2)}) %collective-permute-start.7) | collective-permute-done | bytes 786464 | tf_op jit(solution)/shard_map/ppermute | solution.py:912
  434.1 2.5 collective-permute-start.2
  436.6 0.0 collective-permute-done.6.r13_hbm
  436.6 18.4 %shard_map.140 = (f32[2,384,3072]{2,1,0:T(8,128)}, f32[2,384,3072]{2,1,0:T(8,128)}, f32[2,3072,384]{2,1,0:T(8,128)}) custom-call(s32[8,128]{1,0:T(8,128)S(1)} %get-tuple-element.1677, s32[5]{0:T(128)} %get-tuple-element.929.prm_ref, bf16[8,640,768]{2,1,0:T(8,128)(2,1)} %get-tuple-element.773.u_hbm, ...), custom_call_target="tpu_custom_call", output_to_operand_aliasing={{0}: (9, {}), {1}: (10, {}), {2}: (11, {})} | custom-call | flops 9059696640 | bytes 10485760 | tf_op jit(solution)/shard_map/pallas_call | solution.py:871
  455.0 52.7 %collective-permute-done.5.r2_hbm = bf16[1024,384]{1,0:T(8,128)(2,1)} collective-permute-done((bf16[1024,384]{1,0:T(8,128)(2,1)}, bf16[1024,384]{1,0:T(8,128)(2,1)}, u32[]{:S(2)}, u32[]{:S(2)}) %collective-permute-start.5) | collective-permute-done | bytes 786464 | tf_op jit(solution)/shard_map/ppermute | solution.py:912
  507.7 0.0 collective-permute-done.4.r13_hbm
  507.7 18.6 %shard_map.141 = (f32[2,384,3072]{2,1,0:T(8,128)}, f32[2,384,3072]{2,1,0:T(8,128)}, f32[2,3072,384]{2,1,0:T(8,128)}) custom-call(s32[8,128]{1,0:T(8,128)S(1)} %get-tuple-element.1677, s32[5]{0:T(128)} %get-tuple-element.929.prm_ref, bf16[8,640,768]{2,1,0:T(8,128)(2,1)} %get-tuple-element.773.u_hbm, ...), custom_call_target="tpu_custom_call", output_to_operand_aliasing={{0}: (9, {}), {1}: (10, {}), {2}: (11, {})} | custom-call | flops 9059696640 | bytes 10485760 | tf_op jit(solution)/shard_map/pallas_call | solution.py:871
  526.3 8.6 %collective-permute-done.3.r2_hbm = bf16[1024,384]{1,0:T(8,128)(2,1)} collective-permute-done((bf16[1024,384]{1,0:T(8,128)(2,1)}, bf16[1024,384]{1,0:T(8,128)(2,1)}, u32[]{:S(2)}, u32[]{:S(2)}) %collective-permute-start.3) | collective-permute-done | bytes 786464 | tf_op jit(solution)/shard_map/ppermute | solution.py:912
  534.9 33.9 %collective-permute-done.2.r13_hbm = bf16[768,1024]{1,0:T(8,128)(2,1)} collective-permute-done((bf16[768,1024]{1,0:T(8,128)(2,1)}, bf16[768,1024]{1,0:T(8,128)(2,1)}, u32[]{:S(2)}, u32[]{:S(2)}) %collective-permute-start.2) | collective-permute-done | bytes 1572896 | tf_op jit(solution)/shard_map/ppermute | solution.py:911
  568.8 18.8 %shard_map.142 = (f32[2,384,3072]{2,1,0:T(8,128)}, f32[2,384,3072]{2,1,0:T(8,128)}, f32[2,3072,384]{2,1,0:T(8,128)}) custom-call(s32[8,128]{1,0:T(8,128)S(1)} %get-tuple-element.1677, s32[5]{0:T(128)} %get-tuple-element.929.prm_ref, bf16[8,640,768]{2,1,0:T(8,128)(2,1)} %get-tuple-element.773.u_hbm, ...), custom_call_target="tpu_custom_call", output_to_operand_aliasing={{0}: (9, {}), {1}: (10, {}), {2}: (11, {})} | custom-call | flops 9059696640 | bytes 10485760 | tf_op jit(solution)/shard_map/pallas_call | solution.py:871
  587.6 0.0 reduce-scatter.5.cloned.1.call-done
  587.6 12.3 %unpack.1 = bf16[4096,768]{1,0:T(8,128)(2,1)} custom-call(s32[1]{0:T(128)} %bitcast.18.n_ref, s32[8,512]{1,0:T(8,128)} %reshape.74.pos_ref, f32[8,512]{1,0:T(8,128)} %convert_bitcast_fusion.gate_ref, bf16[4096,768]{1,0:T(8,128)(2,1)} %get-tuple-element.772.refs_0_.h_ref, bf16[640,768]{1,0:T(8,128)(2,1)} %bitcast.99, ...), custom_call_target="tpu_custom_call" | custom-call | flops 4026531840 | bytes 12582912 | tf_op jit(solution)/shard_map/unpack/pallas_call | solution.py:153
  600.0 0.0 reduce-scatter.7.cloned.1.call-done
  600.0 98.3 %attn_bwd.1 = bf16[4096,768]{1,0:T(8,128)(2,1)} custom-call(s32[1]{0:T(128)} %bitcast.18.n_ref, s32[8,512]{1,0:T(8,128)} %reshape.74.pos_ref, bf16[640,768]{1,0:T(8,128)(2,1)} %bitcast.106, bf16[7,640,768]{2,1,0:T(8,128)(2,1)} %get-tuple-element.803.more_hbm, bf16[768,2304]{1,0:T(8,128)(2,1)} %get-tuple-element.804.wqkv_hbm, ...), custom_call_target="tpu_custom_call" | custom-call | flops 49999998976 | bytes 62914560 | tf_op jit(solution)/shard_map/attn_bwd/pallas_call | solution.py:563
  698.3 0.6 while.41
  (9 shorter events, 0.0 us)
Async XLA Ops:
  8.0 7.1 %copy-start = (bf16[2,384,3072]{2,1,0:T(8,128)(2,1)S(1)}, bf16[2,384,3072]{2,1,0:T(8,128)(2,1)}, u32[]{:S(2)}) copy-start(bf16[2,384,3072]{2,1,0:T(8,128)(2,1)} %w1_hbm.11) | copy-start | bytes 14155780
  11.8 14.4 %copy-start.5 = (bf16[8,512,1]{1,0,2:T(8,128)(2,1)S(1)}, bf16[8,512,1]{1,0,2:T(8,128)(2,1)}, u32[]{:S(2)}) copy-start(bf16[8,512,1]{1,0,2:T(8,128)(2,1)} %param.22) | copy-start | bytes 24580
  11.8 14.4 %copy-start.2 = (bf16[384,3,12,64]{0,3,2,1:T(8,128)(2,1)S(1)}, bf16[384,3,12,64]{0,3,2,1:T(8,128)(2,1)}, u32[]{:S(2)}) copy-start(bf16[384,3,12,64]{0,3,2,1:T(8,128)(2,1)} %param.15) | copy-start | bytes 5308420
  11.8 277.4 %collective-permute-start.1 = (bf16[1024,384]{1,0:T(8,128)(2,1)}, bf16[1024,384]{1,0:T(8,128)(2,1)}, u32[]{:S(2)}, u32[]{:S(2)}) collective-permute-start(bf16[1024,384]{1,0:T(8,128)(2,1)} %get-tuple-element.918), channel_id=1, source_target_pairs={{0,4},{4,0},{1,5},{5,1},{2,6},{6,2},{3,7},{7,3}} | collective-permute-start | bytes 2359304 | tf_op jit(solution)/shard_map/ppermute | solution.py:912
  22.3 266.9 %collective-permute-start = (bf16[768,1024]{1,0:T(8,128)(2,1)}, bf16[768,1024]{1,0:T(8,128)(2,1)S(1)}, u32[]{:S(2)}, u32[]{:S(2)}) collective-permute-start(bf16[768,1024]{1,0:T(8,128)(2,1)} %pad_maximum_fusion), channel_id=1, source_target_pairs={{0,4},{4,0},{1,5},{5,1},{2,6},{6,2},{3,7},{7,3}} | collective-permute-start | bytes 4718600 | tf_op jit(solution)/shard_map/ppermute | solution.py:911
  24.9 247.0 %copy-start.3 = (s32[32,128]{1,0:T(8,128)}, s32[32,128]{1,0:T(8,128)S(1)}, u32[]{:S(2)}) copy-start(s32[32,128]{1,0:T(8,128)S(1)} %get-tuple-element.1574) | copy-start | bytes 49156
  311.1 276.5 %reduce-scatter.5.cloned.1.call-start = ((), (), s32[]{:S(2)}) async-start(), calls=%async_computation.4 | async-start | bytes 8847360 | tf_op jit(solution)/shard_map/reduce_scatter | solution.py:949
  311.6 3.4 copy-start.1
  311.7 288.3 %reduce-scatter.7.cloned.1.call-start = ((), (), s32[]{:S(2)}) async-start(), calls=%async_computation.5 | async-start | bytes 8847360 | tf_op jit(solution)/shard_map/reduce_scatter | solution.py:947
  312.3 45.4 %copy-start.4 = (s32[32,128]{1,0:T(8,128)S(1)}, s32[32,128]{1,0:T(8,128)}, u32[]{:S(2)}) copy-start(s32[32,128]{1,0:T(8,128)} %get-tuple-element.1679) | copy-start | bytes 49156
  315.1 45.6 %copy-start.6 = (bf16[8,512,1]{1,0,2:T(8,128)(2,1)S(1)}, bf16[8,512,1]{1,0,2:T(8,128)(2,1)}, u32[]{:S(2)}) copy-start(bf16[8,512,1]{1,0,2:T(8,128)(2,1)} %param.22) | copy-start | bytes 24580
  317.4 119.2 %collective-permute-start.6 = (bf16[768,1024]{1,0:T(8,128)(2,1)}, bf16[768,1024]{1,0:T(8,128)(2,1)S(1)}, u32[]{:S(2)}, u32[]{:S(2)}) collective-permute-start(bf16[768,1024]{1,0:T(8,128)(2,1)} %pad_maximum_fusion.3), channel_id=1, source_target_pairs={{0,4},{4,0},{1,5},{5,1},{2,6},{6,2},{3,7},{7,3}} | collective-permute-start | bytes 4718600 | tf_op jit(solution)/shard_map/ppermute | solution.py:911
  352.4 81.7 %collective-permute-start.7 = (bf16[1024,384]{1,0:T(8,128)(2,1)}, bf16[1024,384]{1,0:T(8,128)(2,1)}, u32[]{:S(2)}, u32[]{:S(2)}) collective-permute-start(bf16[1024,384]{1,0:T(8,128)(2,1)} %get-tuple-element.915), channel_id=1, source_target_pairs={{0,4},{4,0},{1,5},{5,1},{2,6},{6,2},{3,7},{7,3}} | collective-permute-start | bytes 2359304 | tf_op jit(solution)/shard_map/ppermute | solution.py:912
  353.7 154.0 %collective-permute-start.4 = (bf16[768,1024]{1,0:T(8,128)(2,1)}, bf16[768,1024]{1,0:T(8,128)(2,1)S(1)}, u32[]{:S(2)}, u32[]{:S(2)}) collective-permute-start(bf16[768,1024]{1,0:T(8,128)(2,1)} %pad_maximum_fusion.2), channel_id=1, source_target_pairs={{0,4},{4,0},{1,5},{5,1},{2,6},{6,2},{3,7},{7,3}} | collective-permute-start | bytes 4718600 | tf_op jit(solution)/shard_map/ppermute | solution.py:911
  355.7 152.0 %collective-permute-start.5 = (bf16[1024,384]{1,0:T(8,128)(2,1)}, bf16[1024,384]{1,0:T(8,128)(2,1)}, u32[]{:S(2)}, u32[]{:S(2)}) collective-permute-start(bf16[1024,384]{1,0:T(8,128)(2,1)} %get-tuple-element.916), channel_id=1, source_target_pairs={{0,4},{4,0},{1,5},{5,1},{2,6},{6,2},{3,7},{7,3}} | collective-permute-start | bytes 2359304 | tf_op jit(solution)/shard_map/ppermute | solution.py:912
  355.7 179.2 %collective-permute-start.3 = (bf16[1024,384]{1,0:T(8,128)(2,1)}, bf16[1024,384]{1,0:T(8,128)(2,1)}, u32[]{:S(2)}, u32[]{:S(2)}) collective-permute-start(bf16[1024,384]{1,0:T(8,128)(2,1)} %get-tuple-element.917), channel_id=1, source_target_pairs={{0,4},{4,0},{1,5},{5,1},{2,6},{6,2},{3,7},{7,3}} | collective-permute-start | bytes 2359304 | tf_op jit(solution)/shard_map/ppermute | solution.py:912
  434.1 134.7 %collective-permute-start.2 = (bf16[768,1024]{1,0:T(8,128)(2,1)}, bf16[768,1024]{1,0:T(8,128)(2,1)}, u32[]{:S(2)}, u32[]{:S(2)}) collective-permute-start(bf16[768,1024]{1,0:T(8,128)(2,1)} %pad_maximum_fusion.1), channel_id=1, source_target_pairs={{0,4},{4,0},{1,5},{5,1},{2,6},{6,2},{3,7},{7,3}} | collective-permute-start | bytes 4718600 | tf_op jit(solution)/shard_map/ppermute | solution.py:911
Sparse Core Ops, SparseCore 1:
  314.9 126.3 reduce-scatter.4
  444.5 92.8 reduce-scatter.6

commit v3 on v2

--- a/solution.py
+++ b/solution.py
@@ -164,6 +164,7 @@
 
 
 QUERY_BLOCK = 256
+SOFT_ROWS = 64
 
 
 def peers():
@@ -303,17 +304,9 @@
     return lane < 64 if head == 0 else lane >= 64
 
 
-def causal_tail(values, fill):
-    n, k = values.shape
-    tail = values[:, k - n :]
-    keep = lax.broadcasted_iota(jnp.int32, (n, n), 0) >= lax.broadcasted_iota(jnp.int32, (n, n), 1)
-    tail = jnp.where(keep, tail, fill)
-    return tail if k == n else jnp.concatenate([values[:, : k - n], tail], axis=1)
-
-
 def attn_fwd_kernel(pos_ref, cnt_hbm, dy_hbm, wq_hbm, wo_hbm, gate_hbm, up_hbm, down_hbm, x_ref, *refs):
-    h_ref, u_ref, qkv_ref, ctx_ref, p0_ref, p1_ref, wqkv_out, wo_out, cnt_all, dy_all, u_all, a0, b0, a1, b1 = refs[:15]
-    wqkv, wo, acc, u_pack, sem_a, sem_c, sem_d, sem_u, sem_0, sem_1, sem_w = refs[15:]
+    h_ref, u_ref, qkv_ref, ctx_ref, inv_ref, p0_ref, p1_ref, wqkv_out, wo_out, cnt_all, dy_all, u_all, a0, b0, a1, b1 = refs[:16]
+    wqkv, wo, acc, u_pack, s_scr, bias, sem_a, sem_c, sem_d, sem_u, sem_0, sem_1, sem_w = refs[16:]
     i = pl.program_id(0)
     width = x_ref.shape[1]
     hw = width // 2
@@ -356,6 +349,10 @@
             cp.wait()
         for cp in keep:
             cp.start()
+        acc[...] = jnp.zeros_like(acc)
+        shape = (QUERY_BLOCK, QUERY_BLOCK)
+        keep_it = lax.broadcasted_iota(jnp.int32, shape, 0) >= lax.broadcasted_iota(jnp.int32, shape, 1)
+        bias[...] = jnp.where(keep_it, 0.0, -1e30)
 
     @pl.when(i == 2)
     def _():
@@ -379,25 +376,53 @@
     for t in range(3):
         cols = slice(t * width, (t + 1) * width)
         qkv_ref[:, cols] = mm(normed, wqkv[:, cols]).astype(BF16)
-    for pair in range(width // 128):
-        lanes = slice(pair * 128, (pair + 1) * 128)
-        q = qkv_ref[:, lanes] * jnp.asarray(0.125, BF16)
-        k = qkv_ref[:, width + pair * 128 : width + (pair + 1) * 128]
-        v = qkv_ref[:, 2 * width + pair * 128 : 2 * width + (pair + 1) * 128]
-        for j in range(seq // QUERY_BLOCK):
-            rows = slice(j * QUERY_BLOCK, (j + 1) * QUERY_BLOCK)
-            keys = slice(0, (j + 1) * QUERY_BLOCK)
-            outs = []
-            for head in range(2):
-                qm = jnp.where(head_lanes((QUERY_BLOCK, 128), 1, head), q[rows], jnp.zeros((), BF16))
-                s = causal_tail(mm(qm, k[keys], NT), -1e30)
-                top = jnp.max(s, axis=1, keepdims=True)
-                e = jnp.exp(s - top)
-                total = jnp.sum(e, axis=1, keepdims=True)
-                p = (e * (1.0 / total)).astype(BF16)
-                (p0_ref, p1_ref)[j][0, pair * 2 + head] = p
-                outs.append(mm(p, v[keys]))
-            ctx_ref[rows, lanes] = jnp.where(head_lanes((QUERY_BLOCK, 128), 1, 0), outs[0], outs[1]).astype(BF16)
+    units = [(pair, j, head) for pair in range(width // 128) for j in range(2) for head in range(2)]
+    ones = jnp.ones((2 * QUERY_BLOCK, 128), BF16)
+
+    def score(n):
+        pair, j, head = units[n]
+        rows = slice(j * QUERY_BLOCK, (j + 1) * QUERY_BLOCK)
+        keys = slice(0, (j + 1) * QUERY_BLOCK)
+        q = qkv_ref[rows, pair * 128 : (pair + 1) * 128] * jnp.asarray(0.125, BF16)
+        q = jnp.where(head_lanes((QUERY_BLOCK, 128), 1, head), q, jnp.zeros((), BF16))
+        k = qkv_ref[keys, width + pair * 128 : width + (pair + 1) * 128]
+        s_scr[n % 2, :, keys] = mm(q, k, NT)
+
+    def soften(n):
+        pair, j, head = units[n]
+        p_ref = (p0_ref, p1_ref)[j]
+        base = j * QUERY_BLOCK
+        for r in range(0, QUERY_BLOCK, SOFT_ROWS):
+            rows = slice(r, r + SOFT_ROWS)
+            end = (r + SOFT_ROWS + 127) // 128 * 128
+            s = s_scr[n % 2, rows, base : base + end] + bias[rows, :end]
+            if j:
+                s = jnp.concatenate([s_scr[n % 2, rows, :base], s], axis=1)
+            p_ref[0, pair * 2 + head, rows, : base + end] = jnp.exp(s - jnp.max(s, axis=1, keepdims=True)).astype(BF16)
+            if end < QUERY_BLOCK:
+                p_ref[0, pair * 2 + head, rows, base + end :] = jnp.zeros((SOFT_ROWS, QUERY_BLOCK - end), BF16)
+
+    def weigh(n):
+        pair, j, head = units[n]
+        keys = slice(0, (j + 1) * QUERY_BLOCK)
+        v = qkv_ref[keys, 2 * width + pair * 128 : 2 * width + (pair + 1) * 128]
+        both = mm((p0_ref, p1_ref)[j][0, pair * 2 + head], jnp.concatenate([v, ones[keys]], axis=1))
+        return both[:, :128], both[:, 128:]
+
+    score(0)
+    for n, (pair, j, head) in enumerate(units):
+        if n + 1 < len(units):
+            score(n + 1)
+        soften(n)
+        if head == 0:
+            first_out = weigh(n)
+        else:
+            rows, lanes = slice(j * QUERY_BLOCK, (j + 1) * QUERY_BLOCK), slice(pair * 128, (pair + 1) * 128)
+            out, total = weigh(n)
+            left = head_lanes((QUERY_BLOCK, 128), 1, 0)
+            inv = 1.0 / jnp.where(left, first_out[1], total)
+            inv_ref[rows, lanes] = inv
+            ctx_ref[rows, lanes] = (jnp.where(left, first_out[0], out) * inv).astype(BF16)
     ctx = ctx_ref[...]
     for f in range(2):
         cols = slice(f * hw, (f + 1) * hw)
@@ -406,15 +431,7 @@
     u = (h * inv_rms_of(h)).astype(BF16)
     u_ref[...] = u
     hit = lax.broadcasted_iota(jnp.int32, (CHUNK, seq), 0) == pos_ref[pl.ds(i, 1), :]
-    part = mm(jnp.where(hit, 1.0, 0.0).astype(BF16), u)
-
-    @pl.when(i == 0)
-    def _():
-        acc[...] = part
-
-    @pl.when(i > 0)
-    def _():
-        acc[...] += part
+    acc[...] += mm(jnp.where(hit, 1.0, 0.0).astype(BF16), u)
 
     @pl.when(i == pl.num_programs(0) - 1)
     def _():
@@ -444,7 +461,7 @@
     rows = pl.BlockSpec((seq, width), lambda i: (i, 0))
     part = [jax.ShapeDtypeStruct((width, size), BF16), jax.ShapeDtypeStruct((size, hw), BF16)]
     sems = lambda k: pltpu.SemaphoreType.DMA((2, k))
-    h, u, qkv, ctx, p0, p1, *rest = pl.pallas_call(
+    h, u, qkv, ctx, inv, p0, p1, *rest = pl.pallas_call(
         attn_fwd_kernel,
         grid=(n_seq,),
         out_shape=(
@@ -452,6 +469,7 @@
             jax.ShapeDtypeStruct((n, width), BF16),
             jax.ShapeDtypeStruct((n, 3 * width), BF16),
             jax.ShapeDtypeStruct((n, width), BF16),
+            jax.ShapeDtypeStruct((n, width), F32),
             *probs_shapes(n_seq, width),
             jax.ShapeDtypeStruct((width, 3 * width), BF16),
             jax.ShapeDtypeStruct((2, width, hw), BF16),
@@ -462,12 +480,14 @@
             *part,
         ),
         in_specs=[pl.BlockSpec((n_seq, seq), lambda i: (0, 0))] + [ANY] * 7 + [rows],
-        out_specs=(rows, rows, pl.BlockSpec((seq, 3 * width), lambda i: (i, 0)), rows, *probs_specs(width)) + (ANY,) * 9,
+        out_specs=(rows, rows, pl.BlockSpec((seq, 3 * width), lambda i: (i, 0)), rows, rows, *probs_specs(width)) + (ANY,) * 9,
         scratch_shapes=[
             pltpu.VMEM((width, 3 * width), BF16),
             pltpu.VMEM((2, width, hw), BF16),
             pltpu.VMEM((CHUNK, width), F32),
             pltpu.VMEM((CHUNK, width), BF16),
+            pltpu.VMEM((2, QUERY_BLOCK, seq), F32),
+            pltpu.VMEM((QUERY_BLOCK, QUERY_BLOCK), F32),
             sems(8),
             sems(8),
             sems(8),
@@ -480,7 +500,7 @@
         cost_estimate=pl.CostEstimate(flops=30 * 10**9, bytes_accessed=50 * 2**20, transcendentals=0),
         name='attn_fwd',
     )(pos.reshape(n_seq, seq), cnt, dy, wq, wo, *own, x)
-    return (h, u, qkv, ctx, (p0, p1)), rest
+    return (h, u, qkv, ctx, (inv, p0, p1)), rest
 
 
 def norm_back(grad, wide_vals):
@@ -488,7 +508,7 @@
     return inv * (grad - wide_vals * (inv * inv * jnp.mean(grad * wide_vals, axis=-1, keepdims=True)))
 
 
-def attn_bwd_kernel(n_ref, pos_ref, first_ref, more_hbm, wqkv_hbm, wo_hbm, x_ref, h_ref, dout_ref, qkv_ref, ctx_ref, p0_ref, p1_ref, dx_ref, wqkv, wo, dqkv, dctx, dh, buf, sem, w_sem):
+def attn_bwd_kernel(n_ref, pos_ref, first_ref, more_hbm, wqkv_hbm, wo_hbm, x_ref, h_ref, dout_ref, qkv_ref, ctx_ref, inv_ref, p0_ref, p1_ref, dx_ref, wqkv, wo, dqkv, dctx, dp_scr, ds_scr, dh, buf, sem, w_sem):
     i = pl.program_id(0)
     seq, width = x_ref.shape
     hw = width // 2
@@ -515,43 +535,62 @@
     lax.fori_loop(1, n_ref[0], more, 0)
     dh[...] = dout_ref[...].astype(F32) + norm_back(dh[...], h_ref[...].astype(F32))
     dh_b = dh[...].astype(BF16)
-    dctx[...] = (mm(dh_b[:, :hw], wo[0], NT) + mm(dh_b[:, hw:], wo[1], NT)).astype(BF16)
+    dctx[...] = ((mm(dh_b[:, :hw], wo[0], NT) + mm(dh_b[:, hw:], wo[1], NT)) * inv_ref[...]).astype(BF16)
     zero = jnp.zeros((), BF16)
-    for pair in range(width // 128):
-        lanes = slice(pair * 128, (pair + 1) * 128)
-        k_lanes = slice(width + pair * 128, width + (pair + 1) * 128)
-        v_lanes = slice(2 * width + pair * 128, 2 * width + (pair + 1) * 128)
-        q = qkv_ref[:, lanes] * jnp.asarray(0.125, BF16)
-        k, v = qkv_ref[:, k_lanes], qkv_ref[:, v_lanes]
-        do = dctx[:, lanes]
-        q_t, do_t = q.T, do.T
-        prod = do.astype(F32) * ctx_ref[:, lanes].astype(F32)
-        dk_t = [jnp.zeros((128, QUERY_BLOCK), F32) for _ in range(seq // QUERY_BLOCK)]
-        dv_t = list(dk_t)
-        for j in range(seq // QUERY_BLOCK):
-            rows = slice(j * QUERY_BLOCK, (j + 1) * QUERY_BLOCK)
-            keys = slice(0, (j + 1) * QUERY_BLOCK)
-            dqs = []
-            for head in range(2):
-                mine = head_lanes((QUERY_BLOCK, 128), 1, head)
-                mine_t = head_lanes((128, QUERY_BLOCK), 0, head)
-                dom = jnp.where(mine, do[rows], zero)
-                delta = jnp.sum(jnp.where(mine, prod[rows], 0.0), axis=1, keepdims=True)
-                pb = (p0_ref, p1_ref)[j][0, pair * 2 + head]
-                dp = mm(dom, v[keys], NT)
-                ds = (pb.astype(F32) * (dp - delta)).astype(BF16)
-                dqs.append(mm(ds, k[keys]))
-                qm_t, dom_t = jnp.where(mine_t, q_t[:, rows], zero), jnp.where(mine_t, do_t[:, rows], zero)
-                dk_part, dv_part = mm(qm_t, ds), mm(dom_t, pb)
-                for c in range(j + 1):
-                    cols = slice(c * QUERY_BLOCK, (c + 1) * QUERY_BLOCK)
-                    dk_t[c] = dk_t[c] + dk_part[:, cols]
-                    dv_t[c] = dv_t[c] + dv_part[:, cols]
-            dqkv[rows, lanes] = (jnp.where(head_lanes((QUERY_BLOCK, 128), 1, 0), dqs[0], dqs[1]) * 0.125).astype(BF16)
-        for c in range(seq // QUERY_BLOCK):
-            rows = slice(c * QUERY_BLOCK, (c + 1) * QUERY_BLOCK)
-            dqkv[rows, k_lanes] = dk_t[c].astype(BF16).T
-            dqkv[rows, v_lanes] = dv_t[c].astype(BF16).T
+    units = [(pair, j, head) for pair in range(width // 128) for j in range(2) for head in range(2)]
+
+    def third(t, pair):
+        return slice(t * width + pair * 128, t * width + (pair + 1) * 128)
+
+    def block(j):
+        return slice(j * QUERY_BLOCK, (j + 1) * QUERY_BLOCK), slice(0, (j + 1) * QUERY_BLOCK)
+
+    def d_probs(n):
+        pair, j, head = units[n]
+        rows, keys = block(j)
+        do = jnp.where(head_lanes((QUERY_BLOCK, 128), 1, head), dctx[rows, third(0, pair)], zero)
+        dp_scr[n % 2, :, keys] = mm(do, qkv_ref[keys, third(2, pair)], NT)
+
+    def d_scores(n):
+        pair, j, head = units[n]
+        for r in range(0, QUERY_BLOCK, SOFT_ROWS):
+            rows, at = slice(r, r + SOFT_ROWS), slice(j * QUERY_BLOCK + r, j * QUERY_BLOCK + r + SOFT_ROWS)
+            base = j * QUERY_BLOCK
+            end = base + (r + SOFT_ROWS + 127) // 128 * 128
+            prod = dctx[at, third(0, pair)].astype(F32) * ctx_ref[at, third(0, pair)].astype(F32)
+            delta = jnp.sum(jnp.where(head_lanes((SOFT_ROWS, 128), 1, head), prod, 0.0), axis=1, keepdims=True)
+            p = (p0_ref, p1_ref)[j][0, pair * 2 + head, rows, :end].astype(F32)
+            ds_scr[n % 2, rows, :end] = (p * (dp_scr[n % 2, rows, :end] - delta)).astype(BF16)
+            if end < base + QUERY_BLOCK:
+                ds_scr[n % 2, rows, end : base + QUERY_BLOCK] = jnp.zeros((SOFT_ROWS, base + QUERY_BLOCK - end), BF16)
+
+    d_probs(0)
+    for n, (pair, j, head) in enumerate(units):
+        if n + 1 < len(units):
+            d_probs(n + 1)
+        d_scores(n)
+        rows, keys = block(j)
+        if j == 0 and head == 0:
+            q_t = (qkv_ref[:, third(0, pair)] * jnp.asarray(0.125, BF16)).T
+            do_t = dctx[:, third(0, pair)].T
+            dk_t = [jnp.zeros((128, QUERY_BLOCK), F32) for _ in range(2)]
+            dv_t = list(dk_t)
+        ds = ds_scr[n % 2, :, keys]
+        dq = mm(ds, qkv_ref[keys, third(1, pair)])
+        mine_t = head_lanes((128, QUERY_BLOCK), 0, head)
+        dk_part = mm(jnp.where(mine_t, q_t[:, rows], zero), ds)
+        dv_part = mm(jnp.where(mine_t, do_t[:, rows], zero), (p0_ref, p1_ref)[j][0, pair * 2 + head])
+        for c in range(j + 1):
+            dk_t[c] = dk_t[c] + dk_part[:, block(c)[0]]
+            dv_t[c] = dv_t[c] + dv_part[:, block(c)[0]]
+        if head == 0:
+            first_dq = dq
+        else:
+            dqkv[rows, third(0, pair)] = (jnp.where(head_lanes((QUERY_BLOCK, 128), 1, 0), first_dq, dq) * 0.125).astype(BF16)
+            if j == 1:
+                for c in range(2):
+                    dqkv[block(c)[0], third(1, pair)] = dk_t[c].astype(BF16).T
+                    dqkv[block(c)[0], third(2, pair)] = dv_t[c].astype(BF16).T
     dn = mm(dqkv[...], wqkv[...], NT)
     dx_ref[...] = (dh[...] + norm_back(dn, x_ref[...].astype(F32))).astype(BF16)
 
@@ -564,13 +603,15 @@
         attn_bwd_kernel,
         grid=(n_seq,),
         out_shape=jax.ShapeDtypeStruct((n, width), BF16),
-        in_specs=[SMEM, pl.BlockSpec((n_seq, seq), lambda i: (0, 0)), pl.BlockSpec((CHUNK, width), lambda i: (0, 0)), ANY, ANY, ANY, rows, rows, rows, pl.BlockSpec((seq, 3 * width), lambda i: (i, 0)), rows, *probs_specs(width)],
+        in_specs=[SMEM, pl.BlockSpec((n_seq, seq), lambda i: (0, 0)), pl.BlockSpec((CHUNK, width), lambda i: (0, 0)), ANY, ANY, ANY, rows, rows, rows, pl.BlockSpec((seq, 3 * width), lambda i: (i, 0)), rows, rows, *probs_specs(width)],
         out_specs=rows,
         scratch_shapes=[
             pltpu.VMEM((width, 3 * width), BF16),
             pltpu.VMEM((2, width, width // 2), BF16),
             pltpu.VMEM((seq, 3 * width), BF16),
             pltpu.VMEM((seq, width), BF16),
+            pltpu.VMEM((2, QUERY_BLOCK, seq), F32),
+            pltpu.VMEM((2, QUERY_BLOCK, seq), BF16),
             pltpu.VMEM((seq, width), F32),
             pltpu.VMEM((CHUNK, width), BF16),
             pltpu.SemaphoreType.DMA,

time: 711 us -> 720 us (1.013)
    pallas_call x6, Pallas kernels: 111 us -> 126 us  [experts(): pl.pallas_call(functools.partial(experts_kernel, back, first, last, part...]
    pallas_call x1, Pallas kernels: 98.3 us -> 87.3 us  [attn_bwd(): pl.pallas_call(attn_bwd_kernel, grid=(n_seq,), out_shape=jax.ShapeDtypeSt...]
  transfers between devices with their start and end apart: 10 -> 10, of which waited for: 4 -> 4; matrix products, arithmetic and copies ran while one was open for 3% -> 3% of each run, Pallas kernels for 47% -> 46%
where the time goes in v3:
time: 720 us; the launch traced here: 711 us
  Pallas kernels  453 us (63%)
  waiting for transfers between devices  169 us (23%)
  starting transfers between devices  45.2 us (6%)
  local copies, waits for them, and re-layouts  17.2 us (2%)
  between operations  16.1 us (2%)
  other arithmetic  8.81 us (1%)
    pallas_call x1, Pallas kernels, attn_fwd(): pl.pallas_call(attn_fwd_kernel, grid=(n_seq,), out_shape=(jax.ShapeDtypeS...  217 us
    ppermute x4, waiting for transfers between devices, other(): return (both, lax.ppermute(down[cols], 'fsdp', swap))  134 us
    pallas_call x6, Pallas kernels, experts(): pl.pallas_call(functools.partial(experts_kernel, back, first, last, part...  126 us
    pallas_call x1, Pallas kernels, attn_bwd(): pl.pallas_call(attn_bwd_kernel, grid=(n_seq,), out_shape=jax.ShapeDtypeSt...  87.3 us
    ppermute x4, starting transfers between devices, other(): lax.ppermute(jnp.concatenate([gate[:, cols], up[:, cols]], axis=0), 'fsdp...  39.7 us
    ppermute x4, waiting for transfers between devices, other(): lax.ppermute(jnp.concatenate([gate[:, cols], up[:, cols]], axis=0), 'fsdp...  34 us
  transfers between devices with their start and end apart: 10, of which 4 were waited for; matrix products, arithmetic and copies ran while one was open for 3% of the time, Pallas kernels for 46%

profile of v3, /device:TPU:0, one launch (start us, length us, event | category | flops | bytes accessed | tf_op | source)
XLA Modules:
  0.0 711.3 jit_solution(13949162007723375832)
XLA Ops:
  8.0 0.0 copy-start
  8.0 3.7 dynamic-slice_bitcast_fusion.4
  11.7 0.0 copy-start.5
  11.7 0.0 copy-start.2
  11.7 3.3 collective-permute-start.1
  15.1 0.0 copy-done
  15.1 5.8 dynamic-slice_bitcast_fusion
  20.9 0.1 slice.69
  20.9 0.1 slice.68
  21.0 1.3 pad_maximum_fusion
  22.3 0.3 collective-permute-start
  22.6 2.4 route.1
  25.0 0.6 reshape.74.pos_ref
  25.6 0.6 reshape.75.pos_ref
  26.2 0.0 copy-done.5
  26.2 0.0 copy-done.2
  26.3 2.4 copy.64.wq_hbm
  28.6 8.0 %pack.21.dy_hbm = bf16[640,768]{1,0:T(8,128)(2,1)} custom-call(s32[1]{0:T(128)} %constant.118.clone.1.c_ref, s32[4,1024]{1,0:T(4,128)} %reshape.75.pos_ref, f32[4,1024]{1,0:T(4,128)S(1)} %reshape.84.gate_ref, bf16[4096,768]{1,0:T(8,128)(2,1)} %bitcast.104), custom_call_target="tpu_custom_call" | custom-call | flops 4026531840 | bytes 6291456 | tf_op jit(solution)/shard_map/pack/pallas_call | solution.py:101
  36.6 0.6 pad_add_fusion
  37.2 216.8 %attn_fwd.1 = (bf16[4096,768]{1,0:T(8,128)(2,1)}, bf16[4096,768]{1,0:T(8,128)(2,1)}, bf16[4096,2304]{1,0:T(8,128)(2,1)}, bf16[4096,768]{1,0:T(8,128)(2,1)}, f32[...) custom-call(s32[8,512]{1,0:T(8,128)} %reshape.74.pos_ref, ...), custom_call_target="tpu_custom_call" | custom-call | flops 30000001024 | bytes 52428800 | tf_op jit(solution)/shard_map/attn_fwd/pallas_call | solution.py:464
  254.0 18.0 %shard_map.137 = (f32[2,384,3072]{2,1,0:T(8,128)}, f32[2,384,3072]{2,1,0:T(8,128)}, f32[2,3072,384]{2,1,0:T(8,128)}, f32[5120,768]{1,0:T(8,128)}, f32[5120,768]{1,0:T(8,128)}) custom-call(s32[8,128]{1,0:T(8,128)S(1)} %bitcast.93, s32[5]{0:T(128)} %get-tuple-element.932.prm_ref, ...), custom_call_target="tpu_custom_call", output_to_operand_aliasing={{0}: (9, {}), {1}: (10, {}), {2}: (11, {}), {3}: (12, {}), ... | custom-call | flops 15099494400 | bytes 10485760 | tf_op jit(solution)/shard_map/pallas_call | solution.py:912
  272.0 0.1 fusion.1
  272.2 0.0 copy-done.3
  272.2 0.7 fusion.3
  272.9 16.6 %shard_map.138 = (f32[2,384,3072]{2,1,0:T(8,128)}, f32[2,384,3072]{2,1,0:T(8,128)}, f32[2,3072,384]{2,1,0:T(8,128)}, f32[5120,768]{1,0:T(8,128)}, f32[5120,768]{1,0:T(8,128)}) custom-call(s32[8,128]{1,0:T(8,128)S(1)} %bitcast.95, s32[5]{0:T(128)} %get-tuple-element.932.prm_ref, ...), custom_call_target="tpu_custom_call", output_to_operand_aliasing={{0}: (9, {}), {1}: (10, {}), {2}: (11, {}), {3}: (12, {}), ... | custom-call | flops 15099494400 | bytes 10485760 | tf_op jit(solution)/shard_map/pallas_call | solution.py:912
  289.5 0.0 collective-permute-done.1.r2_hbm
  289.5 0.0 collective-permute-done.r13_hbm
  289.5 35.7 %shard_map.139 = (f32[2,384,3072]{2,1,0:T(8,128)}, f32[2,384,3072]{2,1,0:T(8,128)}, f32[2,3072,384]{2,1,0:T(8,128)}, f32[5120,768]{1,0:T(8,128)}, f32[5120,768]{...) custom-call(s32[8,128]{1,0:T(8,128)S(1)} %bitcast.96, ...), custom_call_target="tpu_custom_call", output_to_operand_aliasing={{0}: (9, {}), {1}: (10, {}), {2}: (11, {}), {3}: (12, {}), ... | custom-call | flops 15099494400 | bytes 10485760 | tf_op jit(solution)/shard_map/pallas_call | solution.py:912
  325.2 1.1 while.40
  326.3 0.0 reduce-scatter.5.cloned.1.call-start
  326.4 0.5 reduce-scatter.5.cloned.1.call-update
  326.9 0.0 copy-start.1
  326.9 0.0 reduce-scatter.7.cloned.1.call-start
  327.0 0.5 reduce-scatter.7.cloned.1.call-update
  327.5 0.0 copy-start.4
  327.5 2.8 fusion.5
  330.3 0.0 copy-done.1
  330.3 1.1 fusion.4
  331.4 1.3 pad_maximum_fusion.3
  332.7 35.0 %collective-permute-start.6 = (bf16[768,1024]{1,0:T(8,128)(2,1)}, bf16[768,1024]{1,0:T(8,128)(2,1)S(1)}, u32[]{:S(2)}, u32[]{:S(2)}) collective-permute-start(bf16[768,1024]{1,0:T(8,128)(2,1)} %pad_maximum_fusion.3), channel_id=1, source_target_pairs={{0,4},{4,0},{1,5},{5,1},{2,6},{6,2},{3,7},{7,3}} | collective-permute-start | bytes 4718600 | tf_op jit(solution)/shard_map/ppermute | solution.py:952
  367.6 0.0 collective-permute-start.7
  367.7 1.3 pad_maximum_fusion.2
  368.9 2.0 collective-permute-start.4
  370.9 0.0 collective-permute-start.5
  371.0 2.0 collective-permute-start.3
  373.0 0.0 copy-done.4
  373.0 2.9 pad_maximum_fusion.1
  375.9 0.0 copy-done.6
  375.9 0.6 convert_bitcast_fusion.gate_ref
  376.5 72.8 %collective-permute-done.7.r2_hbm = bf16[1024,384]{1,0:T(8,128)(2,1)} collective-permute-done((bf16[1024,384]{1,0:T(8,128)(2,1)}, bf16[1024,384]{1,0:T(8,128)(2,1)}, u32[]{:S(2)}, u32[]{:S(2)}) %collective-permute-start.7) | collective-permute-done | bytes 786464 | tf_op jit(solution)/shard_map/ppermute | solution.py:953
  449.3 2.5 collective-permute-start.2
  451.8 0.0 collective-permute-done.6.r13_hbm
  451.8 18.4 %shard_map.140 = (f32[2,384,3072]{2,1,0:T(8,128)}, f32[2,384,3072]{2,1,0:T(8,128)}, f32[2,3072,384]{2,1,0:T(8,128)}) custom-call(s32[8,128]{1,0:T(8,128)S(1)} %get-tuple-element.1679, s32[5]{0:T(128)} %get-tuple-element.931.prm_ref, bf16[8,640,768]{2,1,0:T(8,128)(2,1)} %get-tuple-element.774.u_hbm, ...), custom_call_target="tpu_custom_call", output_to_operand_aliasing={{0}: (9, {}), {1}: (10, {}), {2}: (11, {})} | custom-call | flops 9059696640 | bytes 10485760 | tf_op jit(solution)/shard_map/pallas_call | solution.py:912
  470.2 52.7 %collective-permute-done.5.r2_hbm = bf16[1024,384]{1,0:T(8,128)(2,1)} collective-permute-done((bf16[1024,384]{1,0:T(8,128)(2,1)}, bf16[1024,384]{1,0:T(8,128)(2,1)}, u32[]{:S(2)}, u32[]{:S(2)}) %collective-permute-start.5) | collective-permute-done | bytes 786464 | tf_op jit(solution)/shard_map/ppermute | solution.py:953
  522.9 0.0 collective-permute-done.4.r13_hbm
  522.9 18.6 %shard_map.141 = (f32[2,384,3072]{2,1,0:T(8,128)}, f32[2,384,3072]{2,1,0:T(8,128)}, f32[2,3072,384]{2,1,0:T(8,128)}) custom-call(s32[8,128]{1,0:T(8,128)S(1)} %get-tuple-element.1679, s32[5]{0:T(128)} %get-tuple-element.931.prm_ref, bf16[8,640,768]{2,1,0:T(8,128)(2,1)} %get-tuple-element.774.u_hbm, ...), custom_call_target="tpu_custom_call", output_to_operand_aliasing={{0}: (9, {}), {1}: (10, {}), {2}: (11, {})} | custom-call | flops 9059696640 | bytes 10485760 | tf_op jit(solution)/shard_map/pallas_call | solution.py:912
  541.5 8.7 %collective-permute-done.3.r2_hbm = bf16[1024,384]{1,0:T(8,128)(2,1)} collective-permute-done((bf16[1024,384]{1,0:T(8,128)(2,1)}, bf16[1024,384]{1,0:T(8,128)(2,1)}, u32[]{:S(2)}, u32[]{:S(2)}) %collective-permute-start.3) | collective-permute-done | bytes 786464 | tf_op jit(solution)/shard_map/ppermute | solution.py:953
  550.2 34.0 %collective-permute-done.2.r13_hbm = bf16[768,1024]{1,0:T(8,128)(2,1)} collective-permute-done((bf16[768,1024]{1,0:T(8,128)(2,1)}, bf16[768,1024]{1,0:T(8,128)(2,1)}, u32[]{:S(2)}, u32[]{:S(2)}) %collective-permute-start.2) | collective-permute-done | bytes 1572896 | tf_op jit(solution)/shard_map/ppermute | solution.py:952
  584.2 18.8 %shard_map.142 = (f32[2,384,3072]{2,1,0:T(8,128)}, f32[2,384,3072]{2,1,0:T(8,128)}, f32[2,3072,384]{2,1,0:T(8,128)}) custom-call(s32[8,128]{1,0:T(8,128)S(1)} %get-tuple-element.1679, s32[5]{0:T(128)} %get-tuple-element.931.prm_ref, bf16[8,640,768]{2,1,0:T(8,128)(2,1)} %get-tuple-element.774.u_hbm, ...), custom_call_target="tpu_custom_call", output_to_operand_aliasing={{0}: (9, {}), {1}: (10, {}), {2}: (11, {})} | custom-call | flops 9059696640 | bytes 10485760 | tf_op jit(solution)/shard_map/pallas_call | solution.py:912
  603.0 0.0 reduce-scatter.5.cloned.1.call-done
  603.0 12.4 %unpack.1 = bf16[4096,768]{1,0:T(8,128)(2,1)} custom-call(s32[1]{0:T(128)} %bitcast.18.n_ref, s32[8,512]{1,0:T(8,128)} %reshape.74.pos_ref, f32[8,512]{1,0:T(8,128)} %convert_bitcast_fusion.gate_ref, bf16[4096,768]{1,0:T(8,128)(2,1)} %get-tuple-element.773.refs_0_.h_ref, bf16[640,768]{1,0:T(8,128)(2,1)} %bitcast.99, ...), custom_call_target="tpu_custom_call" | custom-call | flops 4026531840 | bytes 12582912 | tf_op jit(solution)/shard_map/unpack/pallas_call | solution.py:153
  615.4 0.0 reduce-scatter.7.cloned.1.call-done
  615.4 87.3 %attn_bwd.1 = bf16[4096,768]{1,0:T(8,128)(2,1)} custom-call(s32[1]{0:T(128)} %bitcast.18.n_ref, s32[8,512]{1,0:T(8,128)} %reshape.74.pos_ref, bf16[640,768]{1,0:T(8,128)(2,1)} %bitcast.106, bf16[7,640,768]{2,1,0:T(8,128)(2,1)} %get-tuple-element.804.more_hbm, bf16[768,2304]{1,0:T(8,128)(2,1)} %get-tuple-element.805.wqkv_hbm, ...), custom_call_target="tpu_custom_call" | custom-call | flops 49999998976 | bytes 62914560 | tf_op jit(solution)/shard_map/attn_bwd/pallas_call | solution.py:602
  702.8 0.7 while.41
  (9 shorter events, 0.0 us)
Async XLA Ops:
  8.0 7.1 copy-start
  11.7 14.5 %copy-start.5 = (bf16[8,512,1]{1,0,2:T(8,128)(2,1)S(1)}, bf16[8,512,1]{1,0,2:T(8,128)(2,1)}, u32[]{:S(2)}) copy-start(bf16[8,512,1]{1,0,2:T(8,128)(2,1)} %param.22) | copy-start | bytes 24580
  11.7 14.5 %copy-start.2 = (bf16[384,3,12,64]{0,3,2,1:T(8,128)(2,1)S(1)}, bf16[384,3,12,64]{0,3,2,1:T(8,128)(2,1)}, u32[]{:S(2)}) copy-start(bf16[384,3,12,64]{0,3,2,1:T(8,128)(2,1)} %param.15) | copy-start | bytes 5308420
  11.7 277.7 %collective-permute-start.1 = (bf16[1024,384]{1,0:T(8,128)(2,1)}, bf16[1024,384]{1,0:T(8,128)(2,1)}, u32[]{:S(2)}, u32[]{:S(2)}) collective-permute-start(bf16[1024,384]{1,0:T(8,128)(2,1)} %get-tuple-element.920), channel_id=1, source_target_pairs={{0,4},{4,0},{1,5},{5,1},{2,6},{6,2},{3,7},{7,3}} | collective-permute-start | bytes 2359304 | tf_op jit(solution)/shard_map/ppermute | solution.py:953
  22.3 267.2 %collective-permute-start = (bf16[768,1024]{1,0:T(8,128)(2,1)}, bf16[768,1024]{1,0:T(8,128)(2,1)S(1)}, u32[]{:S(2)}, u32[]{:S(2)}) collective-permute-start(bf16[768,1024]{1,0:T(8,128)(2,1)} %pad_maximum_fusion), channel_id=1, source_target_pairs={{0,4},{4,0},{1,5},{5,1},{2,6},{6,2},{3,7},{7,3}} | collective-permute-start | bytes 4718600 | tf_op jit(solution)/shard_map/ppermute | solution.py:952
  25.0 247.2 %copy-start.3 = (s32[32,128]{1,0:T(8,128)}, s32[32,128]{1,0:T(8,128)S(1)}, u32[]{:S(2)}) copy-start(s32[32,128]{1,0:T(8,128)S(1)} %get-tuple-element.1576) | copy-start | bytes 49156
  326.3 276.7 %reduce-scatter.5.cloned.1.call-start = ((), (), s32[]{:S(2)}) async-start(), calls=%async_computation.4 | async-start | bytes 8847360 | tf_op jit(solution)/shard_map/reduce_scatter | solution.py:990
  326.9 3.4 copy-start.1
  326.9 288.5 %reduce-scatter.7.cloned.1.call-start = ((), (), s32[]{:S(2)}) async-start(), calls=%async_computation.5 | async-start | bytes 8847360 | tf_op jit(solution)/shard_map/reduce_scatter | solution.py:988
  327.5 45.5 %copy-start.4 = (s32[32,128]{1,0:T(8,128)S(1)}, s32[32,128]{1,0:T(8,128)}, u32[]{:S(2)}) copy-start(s32[32,128]{1,0:T(8,128)} %get-tuple-element.1681) | copy-start | bytes 49156
  330.3 45.6 %copy-start.6 = (bf16[8,512,1]{1,0,2:T(8,128)(2,1)S(1)}, bf16[8,512,1]{1,0,2:T(8,128)(2,1)}, u32[]{:S(2)}) copy-start(bf16[8,512,1]{1,0,2:T(8,128)(2,1)} %param.22) | copy-start | bytes 24580
  332.7 119.1 %collective-permute-start.6 = (bf16[768,1024]{1,0:T(8,128)(2,1)}, bf16[768,1024]{1,0:T(8,128)(2,1)S(1)}, u32[]{:S(2)}, u32[]{:S(2)}) collective-permute-start(bf16[768,1024]{1,0:T(8,128)(2,1)} %pad_maximum_fusion.3), channel_id=1, source_target_pairs={{0,4},{4,0},{1,5},{5,1},{2,6},{6,2},{3,7},{7,3}} | collective-permute-start | bytes 4718600 | tf_op jit(solution)/shard_map/ppermute | solution.py:952
  367.6 81.7 %collective-permute-start.7 = (bf16[1024,384]{1,0:T(8,128)(2,1)}, bf16[1024,384]{1,0:T(8,128)(2,1)}, u32[]{:S(2)}, u32[]{:S(2)}) collective-permute-start(bf16[1024,384]{1,0:T(8,128)(2,1)} %get-tuple-element.917), channel_id=1, source_target_pairs={{0,4},{4,0},{1,5},{5,1},{2,6},{6,2},{3,7},{7,3}} | collective-permute-start | bytes 2359304 | tf_op jit(solution)/shard_map/ppermute | solution.py:953
  368.9 154.0 %collective-permute-start.4 = (bf16[768,1024]{1,0:T(8,128)(2,1)}, bf16[768,1024]{1,0:T(8,128)(2,1)S(1)}, u32[]{:S(2)}, u32[]{:S(2)}) collective-permute-start(bf16[768,1024]{1,0:T(8,128)(2,1)} %pad_maximum_fusion.2), channel_id=1, source_target_pairs={{0,4},{4,0},{1,5},{5,1},{2,6},{6,2},{3,7},{7,3}} | collective-permute-start | bytes 4718600 | tf_op jit(solution)/shard_map/ppermute | solution.py:952
  370.9 152.0 %collective-permute-start.5 = (bf16[1024,384]{1,0:T(8,128)(2,1)}, bf16[1024,384]{1,0:T(8,128)(2,1)}, u32[]{:S(2)}, u32[]{:S(2)}) collective-permute-start(bf16[1024,384]{1,0:T(8,128)(2,1)} %get-tuple-element.918), channel_id=1, source_target_pairs={{0,4},{4,0},{1,5},{5,1},{2,6},{6,2},{3,7},{7,3}} | collective-permute-start | bytes 2359304 | tf_op jit(solution)/shard_map/ppermute | solution.py:953
  371.0 179.3 %collective-permute-start.3 = (bf16[1024,384]{1,0:T(8,128)(2,1)}, bf16[1024,384]{1,0:T(8,128)(2,1)}, u32[]{:S(2)}, u32[]{:S(2)}) collective-permute-start(bf16[1024,384]{1,0:T(8,128)(2,1)} %get-tuple-element.919), channel_id=1, source_target_pairs={{0,4},{4,0},{1,5},{5,1},{2,6},{6,2},{3,7},{7,3}} | collective-permute-start | bytes 2359304 | tf_op jit(solution)/shard_map/ppermute | solution.py:953
  449.3 134.8 %collective-permute-start.2 = (bf16[768,1024]{1,0:T(8,128)(2,1)}, bf16[768,1024]{1,0:T(8,128)(2,1)}, u32[]{:S(2)}, u32[]{:S(2)}) collective-permute-start(bf16[768,1024]{1,0:T(8,128)(2,1)} %pad_maximum_fusion.1), channel_id=1, source_target_pairs={{0,4},{4,0},{1,5},{5,1},{2,6},{6,2},{3,7},{7,3}} | collective-permute-start | bytes 4718600 | tf_op jit(solution)/shard_map/ppermute | solution.py:952
Sparse Core Ops, SparseCore 1:
  330.2 126.4 reduce-scatter.4
  459.9 92.8 reduce-scatter.6
